TPU v7x, 128 devices: a whole 4x4x4 slice. The times are simulated.
128 devices in a mesh: rows: 128 (over y, z, x, core).
Axes of the slice: x: 4, y: 4, z: 4, core: 2. Of those that a mesh axis runs over, the one named last changes fastest.
Arguments:
- source: bfloat16 [262144, 128], P('rows'), may hold values from -6 to 6
- target: bfloat16 [262144, 128], P('rows'), may hold values from -6 to 6
- tile_values: bfloat16 [16384, 128, 128], P('rows'), may hold values from -0.25 to 0.25
- tile_rows: int32 [16384], P('rows'), may hold values from 0 to 15
- tile_peers: int32 [16384], P('rows'), may hold values from 0 to 127
- need_list: int32 [128, 128], P('rows'), may hold values from 0 to 15
- tile_count: int32 [128], P('rows'), may hold values from 1 to 128, as said below
Outputs:
- source_embed: bfloat16 [262144, 128], P('rows')
- target_embed: bfloat16 [262144, 128], P('rows')
Inputs may be any that keep to these rules, and one draw needn't show every extreme that they name: `tile_count`: some device has 128 live tiles; tiles in slots at or past the count take no part.
All inputs are finite; a program needn't handle non-finite values.
Results may differ from a plain program's by a relative error of at most 0.0053.
Values may be sent and summed in bfloat16 or wider, within the bound.
No kernel may reach another device: no remote copies, remote signals or barrier semaphores. Data moves between devices by JAX's collectives and lax.ppermute only.
A program may use at most 128 MiB of HBM per device.

v0:
```python
import jax
import jax.numpy as jnp
from jax import lax
from jax.sharding import PartitionSpec as P

ITERS = 2


epsilon = 1e-06


def settle(base, update):
    total = base.astype(jnp.float32) + update
    scale = lax.rsqrt(jnp.mean(total * total, axis=-1, keepdims=True) + epsilon)
    return (total * scale).astype(jnp.bfloat16)


def send_source(outgoing):
    return lax.all_to_all(outgoing, "rows", split_axis=0, concat_axis=0, tiled=True)


def send_partial(partial_value):
    return lax.all_to_all(
        partial_value.astype(jnp.bfloat16), "rows", split_axis=0, concat_axis=0, tiled=True
    ).astype(partial_value.dtype)


def shards(source, target, tile_values, tile_rows, tile_peers, need_list, tile_count):
    peers_total = lax.axis_size("rows")
    tile_side = tile_values.shape[1]
    feature_width = source.shape[1]
    row_count = source.shape[0] // tile_side
    tiles_here = tile_values.shape[0]
    group_size = min(16, tiles_here)
    group_count = tiles_here // group_size
    live_count = tile_count[0]
    wanted = need_list.reshape(peers_total, 1)
    send_list = lax.all_to_all(wanted, "rows", split_axis=0, concat_axis=0, tiled=True)[:, 0]
    owner_hot = (send_list[None, :] == jnp.arange(row_count, dtype=jnp.int32)[:, None]).astype(
        jnp.float32
    )

    def fetch_group(position):
        first_tile = position * group_size
        tile_block = lax.dynamic_slice_in_dim(tile_values, first_tile, group_size, 0)
        row_ids = lax.dynamic_slice_in_dim(tile_rows, first_tile, group_size, 0)
        peer_ids = lax.dynamic_slice_in_dim(tile_peers, first_tile, group_size, 0)
        positions = first_tile + jnp.arange(group_size, dtype=jnp.int32)
        live_mask = (positions < live_count).astype(jnp.float32)[:, None, None]
        return (tile_block, row_ids, peer_ids, live_mask)

    def forward_add(running, fetched, position):
        tile_block, row_ids, peer_ids, live_mask = fetch_group(position)
        product = (
            jnp.einsum(
                "tij,tjk->tik", tile_block, fetched[peer_ids], preferred_element_type=jnp.float32
            )
            * live_mask
        )
        return running.at[row_ids].add(product)

    def backward_add(running, target_blocks, position):
        tile_block, row_ids, peer_ids, live_mask = fetch_group(position)
        product = (
            jnp.einsum(
                "tji,tjk->tik",
                tile_block,
                target_blocks[row_ids],
                preferred_element_type=jnp.float32,
            )
            * live_mask
        )
        return running.at[peer_ids].add(product)

    source_now, target_now = (source, target)
    for iteration in range(ITERS):
        source_blocks = source_now.reshape(row_count, tile_side, feature_width)
        target_blocks = target_now.reshape(row_count, tile_side, feature_width)
        outgoing = source_blocks[send_list]
        empty_rows = jnp.zeros((row_count, tile_side, feature_width), jnp.float32)
        empty_peers = jnp.zeros((peers_total, tile_side, feature_width), jnp.float32)
        partial_value = lax.fori_loop(
            0,
            group_count,
            lambda position, running: backward_add(running, target_blocks, position),
            empty_peers,
        )
        returned = send_partial(partial_value)
        fetched = send_source(outgoing)
        gathered = lax.fori_loop(
            0,
            group_count,
            lambda position, running: forward_add(running, fetched, position),
            empty_rows,
        )
        incoming = jnp.dot(
            owner_hot,
            returned.reshape(peers_total, -1),
            precision=lax.Precision.HIGHEST,
            preferred_element_type=jnp.float32,
        )
        source_now = settle(source, gathered.reshape(-1, feature_width))
        target_now = settle(target, incoming.reshape(-1, feature_width))
    return (source_now, target_now)


def solution(mesh):
    return jax.shard_map(
        shards,
        mesh=mesh,
        in_specs=(
            P("rows", None),
            P("rows", None),
            P("rows", None, None),
            P("rows"),
            P("rows"),
            P("rows", None),
            P("rows"),
        ),
        out_specs=(P("rows", None), P("rows", None)),
        check_vma=False,
    )
```

profile of v0, /device:TPU:0, one launch (start us, length us, event | category | flops | bytes accessed | tf_op | source)
XLA Modules:
  0.0 397.1 jit_solution(15481180898659917192)
XLA Ops:
  2.0 11.2 %all-to-all-start = ((s32[128,1,1]{2,1,0:T(1,128)}), s32[128,1,1]{2,1,0:T(1,128)S(1)}, u32[]{:S(2)}, u32[]{:S(2)}) async-start(s32[128,1,1]{2,1,0:T(1,128)} %copy.14), calls=%async_computation | async-start | bytes 131072 | tf_op jit(solution)/shard_map/all_to_all | solution.py:38
  13.2 6.4 %copy.16 = bf16[128,128,128]{1,2,0:T(8,128)(2,1)} copy(bf16[128,128,128]{2,1,0:T(8,128)(2,1)} %param.17) | data formatting | bytes 8388608 | tf_op jit(solution)/shard_map/while | solution.py:82
  19.6 4.3 %broadcast.213.clone = f32[128,128,128]{2,1,0:T(8,128)} broadcast(f32[]{:T(128)} %constant.137.clone.1), dimensions={} | broadcast | bytes 8388612 | tf_op jit(solution)/shard_map/broadcast.32
  23.8 48.6 %while.54 = (s32[]{:T(128)}, f32[128,128,128]{2,1,0:T(8,128)}, s32[128]{0:T(128)S(1)}, bf16[128,128,128]{1,2,0:T(8,128)(2,1)}, s32[128]{0:T(128)S(1)}, /*index=5...) while((s32[]{:T(128)}, f32[128,128,128]{2,1,0:T(8,128)}, ...), condition=%wide.region_10.0_spmd, body=%wide.region_8.0_spmd.sunk | while | flops 67634328 | bytes 6296299 | solution.py:82
  32.6 3.3 scatter_fusion.2
  38.7 3.4 scatter_fusion.2
  44.8 3.4 scatter_fusion.2
  50.9 3.3 scatter_fusion.2
  56.9 3.3 scatter_fusion.2
  63.0 3.3 scatter_fusion.2
  69.1 3.3 scatter_fusion.2
  72.4 6.3 %convert_element_type.77 = bf16[128,128,128]{2,1,0:T(8,128)(2,1)} convert(f32[128,128,128]{2,1,0:T(8,128)} %get-tuple-element.500) | non-fusion elementwise | flops 2097152 | bytes 12582912 | tf_op jit(solution)/shard_map/convert_element_type | solution.py:24
  78.8 10.4 %all-to-all-start.3 = ((bf16[128,128,128]{2,1,0:T(8,128)(2,1)}), bf16[128,128,128]{2,1,0:T(8,128)(2,1)}, u32[]{:S(2)}, u32[]{:S(2)}) async-start(bf16[128,128,128]{2,1,0:T(8,128)(2,1)} %convert_element_type.77), calls=%async_computation.3 | async-start | bytes 8388608 | tf_op jit(solution)/shard_map/all_to_all | solution.py:23
  94.6 47.0 %all-to-all-done.3 = bf16[128,128,128]{2,1,0:T(8,128)(2,1)} async-done(((bf16[128,128,128]{2,1,0:T(8,128)(2,1)}), bf16[128,128,128]{2,1,0:T(8,128)(2,1)}, u32[]{:S(2)}, u32[]{:S(2)}) %all-to-all-start.3) | async-done | bytes 4194336 | tf_op jit(solution)/shard_map/all_to_all | solution.py:23
  141.6 6.0 %all-to-all-start.1 = ((bf16[128,128,128]{2,1,0:T(8,128)(2,1)}), bf16[128,128,128]{2,1,0:T(8,128)(2,1)}, u32[]{:S(2)}, u32[]{:S(2)}) async-start(bf16[128,128,128]{2,1,0:T(8,128)(2,1)} %gather_fusion.4), calls=%async_computation.1 | async-start | bytes 8388608 | tf_op jit(solution)/shard_map/all_to_all | solution.py:19
  147.6 4.5 %fusion.11 = f32[16,16384]{1,0:T(8,128)S(1)} fusion(bf16[16,8,128,128]{3,2,1,0:T(8,128)(2,1)} %bitcast.10, s32[128]{0:T(128)S(1)} %reduce), kind=kOutput, calls=%fused_computation.41 | convolution fusion | flops 67110912 | bytes 5243392 | tf_op jit(solution)/shard_map/dot_general | solution.py:96
  153.0 4.3 %broadcast.213 = f32[128,128,128]{2,1,0:T(8,128)} broadcast(f32[]{:T(128)} %constant.137.clone.1), dimensions={} | broadcast | bytes 8388612 | tf_op jit(solution)/shard_map/broadcast.32
  157.3 48.5 %while.55 = (s32[]{:T(128)}, f32[128,128,128]{2,1,0:T(8,128)}, s32[128]{0:T(128)S(1)}, bf16[128,128,128]{1,2,0:T(8,128)(2,1)}, s32[128]{0:T(128)S(1)}, /*index=5...) while((s32[]{:T(128)}, f32[128,128,128]{2,1,0:T(8,128)}, ...), condition=%wide.region_14.0_spmd, body=%wide.region_12.14_spmd.sunk | while | flops 67634328 | bytes 6296299 | solution.py:82
  166.1 3.3 scatter_fusion.3
  172.1 3.4 scatter_fusion.3
  178.2 3.4 scatter_fusion.3
  184.3 3.3 scatter_fusion.3
  190.4 3.3 scatter_fusion.3
  196.4 3.3 scatter_fusion.3
  202.5 3.3 scatter_fusion.3
  205.8 6.3 %convert_element_type.79 = bf16[128,128,128]{2,1,0:T(8,128)(2,1)} convert(f32[128,128,128]{2,1,0:T(8,128)} %get-tuple-element.501) | non-fusion elementwise | flops 2097152 | bytes 12582912 | tf_op jit(solution)/shard_map/convert_element_type | solution.py:24
  212.2 10.2 %all-to-all-start.4 = ((bf16[128,128,128]{2,1,0:T(8,128)(2,1)}), bf16[128,128,128]{2,1,0:T(8,128)(2,1)}, u32[]{:S(2)}, u32[]{:S(2)}) async-start(bf16[128,128,128]{2,1,0:T(8,128)(2,1)} %convert_element_type.79), calls=%async_computation.4 | async-start | bytes 8388608 | tf_op jit(solution)/shard_map/all_to_all | solution.py:23
  222.5 52.5 %while.52 = (s32[]{:T(128)}, f32[16,128,128]{2,1,0:T(8,128)S(1)}, s32[128]{0:T(128)S(1)}, bf16[128,128,128]{2,1,0:T(8,128)(2,1)}, s32[128]{0:T(128)S(1)}, /*inde...) while((s32[]{:T(128)}, f32[16,128,128]{2,1,0:T(8,128)S(1)}, ...), condition=%wide.region_2.0_spmd, body=%wide.region_0.0_spmd.sunk | while | flops 67634328 | bytes 6296299 | solution.py:90
  278.8 10.4 %all-to-all-start.2 = ((bf16[128,128,128]{2,1,0:T(8,128)(2,1)}), bf16[128,128,128]{2,1,0:T(8,128)(2,1)}, u32[]{:S(2)}, u32[]{:S(2)}) async-start(bf16[128,128,128]{2,1,0:T(8,128)(2,1)} %gather_fusion.5), calls=%async_computation.2 | async-start | bytes 8388608 | tf_op jit(solution)/shard_map/all_to_all | solution.py:19
  289.3 4.6 %fusion.8 = f32[16,16384]{1,0:T(8,128)S(1)} fusion(bf16[16,8,128,128]{3,2,1,0:T(8,128)(2,1)} %bitcast.12, s32[128]{0:T(128)S(1)} %reduce), kind=kOutput, calls=%fused_computation.38 | convolution fusion | flops 67110912 | bytes 5243392 | tf_op jit(solution)/shard_map/dot_general | solution.py:96
  295.0 46.4 %all-to-all-done.2 = bf16[128,128,128]{2,1,0:T(8,128)(2,1)} async-done(((bf16[128,128,128]{2,1,0:T(8,128)(2,1)}), bf16[128,128,128]{2,1,0:T(8,128)(2,1)}, u32[]{:S(2)}, u32[]{:S(2)}) %all-to-all-start.2) | async-done | bytes 4194336 | tf_op jit(solution)/shard_map/all_to_all | solution.py:19
  341.5 52.5 %while.53 = (s32[]{:T(128)}, f32[16,128,128]{2,1,0:T(8,128)S(1)}, s32[128]{0:T(128)S(1)}, bf16[128,128,128]{2,1,0:T(8,128)(2,1)}, s32[128]{0:T(128)S(1)}, /*inde...) while((s32[]{:T(128)}, f32[16,128,128]{2,1,0:T(8,128)S(1)}, ...), condition=%wide.region_6.0_spmd, body=%wide.region_4.6_spmd.sunk | while | flops 67634328 | bytes 6296299 | solution.py:90
  (214 shorter events, 170.0 us)
Async XLA Ops:
  2.0 76.7 %all-to-all-start = ((s32[128,1,1]{2,1,0:T(1,128)}), s32[128,1,1]{2,1,0:T(1,128)S(1)}, u32[]{:S(2)}, u32[]{:S(2)}) async-start(s32[128,1,1]{2,1,0:T(1,128)} %copy.14), calls=%async_computation | async-start | bytes 131072 | tf_op jit(solution)/shard_map/all_to_all | solution.py:38
  19.6 4.3 %copy-start.1 = (bf16[2048,128]{1,0:T(8,128)(2,1)S(1)}, bf16[2048,128]{1,0:T(8,128)(2,1)}, u32[]{:S(2)}) copy-start(bf16[2048,128]{1,0:T(8,128)(2,1)} %param.16) | copy-start | bytes 1572868
  19.6 4.3 %copy-start.4 = (s32[128]{0:T(128)S(1)}, s32[128]{0:T(128)}, u32[]{:S(2)}) copy-start(s32[128]{0:T(128)} %param.19) | copy-start | bytes 1540
  19.6 4.3 %copy-start.5 = (s32[128]{0:T(128)S(1)}, s32[128]{0:T(128)}, u32[]{:S(2)}) copy-start(s32[128]{0:T(128)} %param.18) | copy-start | bytes 1540
  78.8 12.8 %copy-start = (bf16[2048,128]{1,0:T(8,128)(2,1)S(1)}, bf16[2048,128]{1,0:T(8,128)(2,1)}, u32[]{:S(2)}) copy-start(bf16[2048,128]{1,0:T(8,128)(2,1)} %param.15) | copy-start | bytes 1572868
  78.8 62.9 %all-to-all-start.3 = ((bf16[128,128,128]{2,1,0:T(8,128)(2,1)}), bf16[128,128,128]{2,1,0:T(8,128)(2,1)}, u32[]{:S(2)}, u32[]{:S(2)}) async-start(bf16[128,128,128]{2,1,0:T(8,128)(2,1)} %convert_element_type.77), calls=%async_computation.3 | async-start | bytes 8388608 | tf_op jit(solution)/shard_map/all_to_all | solution.py:23
  141.6 70.6 %all-to-all-start.1 = ((bf16[128,128,128]{2,1,0:T(8,128)(2,1)}), bf16[128,128,128]{2,1,0:T(8,128)(2,1)}, u32[]{:S(2)}, u32[]{:S(2)}) async-start(bf16[128,128,128]{2,1,0:T(8,128)(2,1)} %gather_fusion.4), calls=%async_computation.1 | async-start | bytes 8388608 | tf_op jit(solution)/shard_map/all_to_all | solution.py:19
  212.2 66.6 %all-to-all-start.4 = ((bf16[128,128,128]{2,1,0:T(8,128)(2,1)}), bf16[128,128,128]{2,1,0:T(8,128)(2,1)}, u32[]{:S(2)}, u32[]{:S(2)}) async-start(bf16[128,128,128]{2,1,0:T(8,128)(2,1)} %convert_element_type.79), calls=%async_computation.4 | async-start | bytes 8388608 | tf_op jit(solution)/shard_map/all_to_all | solution.py:23
  278.8 62.6 %all-to-all-start.2 = ((bf16[128,128,128]{2,1,0:T(8,128)(2,1)}), bf16[128,128,128]{2,1,0:T(8,128)(2,1)}, u32[]{:S(2)}, u32[]{:S(2)}) async-start(bf16[128,128,128]{2,1,0:T(8,128)(2,1)} %gather_fusion.5), calls=%async_computation.2 | async-start | bytes 8388608 | tf_op jit(solution)/shard_map/all_to_all | solution.py:19
  289.3 4.7 %copy-start.2 = (bf16[2048,128]{1,0:T(8,128)(2,1)S(1)}, bf16[2048,128]{1,0:T(8,128)(2,1)}, u32[]{:S(2)}) copy-start(bf16[2048,128]{1,0:T(8,128)(2,1)} %param.16) | copy-start | bytes 1572868
  294.0 1.0 copy-start.3
where the time goes:
time: 402 us; the launch traced here: 397 us
  other arithmetic  122 us (30%)
  waiting for transfers between devices  93.5 us (23%)
  local copies, waits for them, and re-layouts  79.2 us (20%)
  matrix products  51.9 us (13%)
  starting transfers between devices  48.3 us (12%)
    scatter-add x16, other arithmetic, backward_add(): return running.at[peer_ids].add(product)  53.2 us
    all_to_all x2, waiting for transfers between devices, send_partial(): lax.all_to_all(partial_value.astype(jnp.bfloat16), 'rows', split_axis=0,...  47 us
    all_to_all x2, waiting for transfers between devices, send_source(): lax.all_to_all(outgoing, 'rows', split_axis=0, concat_axis=0, tiled=True)  46.4 us
    gather x16, local copies, waits for them, and re-layouts, forward_add(): fetched[peer_ids]  45.4 us
    scatter-add x16, other arithmetic, forward_add(): return running.at[row_ids].add(product)  25.7 us
    dot_general x16, matrix products, forward_add(): jnp.einsum('tij,tjk->tik', tile_block, fetched[peer_ids], preferred_eleme...  21.4 us
    dot_general x16, matrix products, backward_add(): jnp.einsum('tji,tjk->tik', tile_block, target_blocks[row_ids], preferred_...  21.4 us
    convert_element_type x32, other arithmetic, fetch_group(): live_mask = (positions < live_count).astype(jnp.float32)[:, None, None]  20.8 us
  transfers between devices with their start and end apart: 5, of which 2 were waited for; matrix products, arithmetic and copies ran while one was open for 49% of the time, Pallas kernels for 0%

commit v1 on v0

v1 whole, which is shorter than its diff:
```python
import functools
import jax
import jax.numpy as jnp
from jax import lax
from jax.experimental import pallas as pl
from jax.experimental.pallas import tpu as pltpu
from jax.sharding import PartitionSpec as P

ITERS = 2
epsilon = 1e-06

SIDE = 128
OWN = 16
CAP = 63
PITCH = OWN + CAP + 1
META = PITCH - 1
F32 = jnp.float32
BF16 = jnp.bfloat16
MIB = 1 << 20


def settle(base, update):
    total = base.astype(F32) + update
    scale = lax.rsqrt(jnp.mean(total * total, axis=-1, keepdims=True) + epsilon)
    return (total * scale).astype(BF16)


def block(ref, index):
    return ref[pl.ds(pl.multiple_of(index * SIDE, SIDE), SIDE), :]


def pack_rows(scr, x_ref, acc, peers, buf):
    for b in range(OWN):
        scr[pl.ds(b, SIDE, stride=PITCH), :] = x_ref[b * SIDE : (b + 1) * SIDE, :].astype(F32)

    def put(c, _):
        scr[pl.ds(OWN + c, SIDE, stride=PITCH), :] = block(acc, c)
        return 0

    lax.fori_loop(0, peers, put, 0)

    def narrow(i, _):
        buf[i] = scr[pl.ds(pl.multiple_of(i * PITCH, 8), PITCH), :].astype(BF16)
        return 0

    lax.fori_loop(0, SIDE, narrow, 0, unroll=4)


def zero(ref, blocks):
    def one(c, _):
        ref[pl.ds(pl.multiple_of(c * SIDE, SIDE), SIDE), :] = jnp.zeros((SIDE, SIDE), F32)
        return 0

    lax.fori_loop(0, blocks, one, 0)


def back_dot(tile, y):
    return lax.dot_general(tile, y, (((0,), (0,)), ((), ())), preferred_element_type=F32)


STEP = 4


def first_kernel(
    count, rows, peers_ref, need_ref, tiles, x_ref, y_ref, buf, slots, scr, acc, slot_v, sem
):
    live = count[0]
    row_at = lax.broadcasted_iota(jnp.int32, (SIDE, SIDE), 0)
    lane_at = lax.broadcasted_iota(jnp.int32, (SIDE, SIDE), 1)
    hit = jnp.where((row_at == peers_ref[...]) & (lane_at < live), 1.0, 0.0)
    used = jnp.broadcast_to(jnp.max(hit, axis=1, keepdims=True), (SIDE, SIDE))
    below = jnp.where(lane_at < row_at, 1.0, 0.0).astype(BF16)
    slot = jnp.dot(below, used.astype(BF16), preferred_element_type=F32)
    total = jnp.sum(used, axis=0, keepdims=True)
    lane = lax.broadcasted_iota(jnp.int32, (1, SIDE), 1)
    mine = jnp.sum(hit * slot, axis=0, keepdims=True)
    mine = jnp.where(lane < live, jnp.minimum(mine, float(CAP)), float(CAP))
    peer_total = jnp.minimum(total, float(CAP))
    slot_v[0:1, :] = mine.astype(jnp.int32)
    slot_v[1:2, :] = peer_total.astype(jnp.int32)
    copy = pltpu.make_async_copy(slot_v, slots, sem)
    copy.start()
    at = jnp.where(used > 0, slot, -1.0)
    pick = at == lane_at.astype(F32)
    peer_of = jnp.sum(jnp.where(pick, row_at.astype(F32), 0.0), axis=0, keepdims=True)
    peer_of = jnp.where(lane.astype(F32) < total, peer_of, float(SIDE))
    need_col = jnp.sum(
        jnp.where(row_at == lane_at, need_ref[...], 0).astype(F32), axis=1, keepdims=True
    )
    pick = (at == (lane_at - CAP - 1).astype(F32)) & (lane_at > CAP)
    need_of = jnp.sum(jnp.where(pick, need_col, 0.0), axis=0, keepdims=True)
    meta = jnp.where(lane < CAP, peer_of, jnp.where(lane == CAP, total, need_of))
    scr[pl.ds(META, SIDE, stride=PITCH), :] = jnp.broadcast_to(meta, (SIDE, SIDE))
    copy.wait()
    peers = slots[1, 0]
    zero(acc, peers)

    def step(g, _):
        parts = []
        for k in range(STEP):
            t = g * STEP + k
            parts.append((slots[0, t], back_dot(tiles[t], block(y_ref, rows[t]))))
        for s, part in parts:
            where = pl.ds(pl.multiple_of(s * SIDE, SIDE), SIDE)
            acc[where, :] = acc[where, :] + part
        return 0

    lax.fori_loop(0, (live + STEP - 1) // STEP, step, 0)
    pack_rows(scr, x_ref, acc, peers, buf)


LANES8 = 8


def middle_kernel(index, counts, recv, buf, xs, acc, parts, outs):
    def load(d, _):
        at = pl.ds(pl.multiple_of(d * OWN, OWN), OWN)
        xs[at, :] = recv[d, 0:OWN, :].astype(F32)
        acc[at, :] = jnp.zeros((OWN, SIDE), F32)
        return 0

    lax.fori_loop(0, SIDE, load, 0, unroll=4)
    xs[OWN * SIDE :, :] = jnp.zeros((8, SIDE), F32)

    def reader(d, _):
        def batch(b, _):
            start = pl.multiple_of(b * LANES8, LANES8)
            parts[pl.ds(start, LANES8), :] = recv[d, pl.ds(OWN + start, LANES8), :].astype(F32)
            spots = [index[d, start + k] for k in range(LANES8)]
            sums = []
            for k, spot in enumerate(spots):
                outs[pl.ds(d * (CAP + 1) + start + k, 1), :] = xs[pl.ds(spot, 1), :]
                sums.append(acc[pl.ds(spot, 1), :] + parts[pl.ds(start + k, 1), :])
            for k, spot in enumerate(spots):
                acc[pl.ds(spot, 1), :] = sums[k]
            return 0

        lax.fori_loop(0, (counts[d] + LANES8 - 1) // LANES8, batch, 0)
        return 0

    lax.fori_loop(0, SIDE, reader, 0)

    def narrow(d, _):
        buf[d, 0:OWN, :] = acc[pl.ds(pl.multiple_of(d * OWN, OWN), OWN), :].astype(BF16)
        at = pl.ds(pl.multiple_of(d * (CAP + 1), CAP + 1), CAP + 1)
        buf[d, OWN:PITCH, :] = outs[at, :].astype(BF16)
        return 0

    lax.fori_loop(0, SIDE, narrow, 0, unroll=4)


def tail_kernel(
    last, count, rows, slots, recv, tiles, source, target, *rest
):
    if last:
        x_new, y_new, scr, xb, acc_x = rest
        buf = acc = None
    else:
        buf, scr, xb, acc_x, acc, x_new, y_new = rest
    live = count[0]
    peers = slots[1, 0]

    def widen(i, _):
        scr[pl.ds(pl.multiple_of(i * PITCH, 8), PITCH), :] = recv[i].astype(F32)
        return 0

    lax.fori_loop(0, SIDE, widen, 0, unroll=4)
    for b in range(OWN):
        at = slice(b * SIDE, (b + 1) * SIDE)
        y_new[at, :] = settle(target[at, :], scr[pl.ds(b, SIDE, stride=PITCH), :])

    def fetch(c, _):
        xb[pl.ds(pl.multiple_of(c * SIDE, SIDE), SIDE), :] = scr[
            pl.ds(OWN + c, SIDE, stride=PITCH), :
        ].astype(BF16)
        return 0

    lax.fori_loop(0, peers, fetch, 0)
    zero(acc_x, OWN)
    if not last:
        zero(acc, peers)

    def step(g, _):
        ahead, back = [], []
        for k in range(STEP):
            t = g * STEP + k
            s, r, tile = slots[0, t], rows[t], tiles[t]
            to = jnp.where(t < live, r, OWN)
            ahead.append((to, jnp.dot(tile, block(xb, s), preferred_element_type=F32)))
            if not last:
                back.append((s, back_dot(tile, block(y_new, r))))
        for ref, found in ((acc_x, ahead), (acc, back)):
            for s, part in found:
                where = pl.ds(pl.multiple_of(s * SIDE, SIDE), SIDE)
                ref[where, :] = ref[where, :] + part
        return 0

    lax.fori_loop(0, (live + STEP - 1) // STEP, step, 0)
    for b in range(OWN):
        at = slice(b * SIDE, (b + 1) * SIDE)
        x_new[at, :] = settle(source[at, :], acc_x[at, :])
    if not last:
        pack_rows(scr, x_new, acc, peers, buf)


def vmem(shape, dtype):
    return pltpu.VMEM(shape, dtype)


IN_VMEM = pl.BlockSpec(memory_space=pltpu.VMEM)
IN_SMEM = pl.BlockSpec(memory_space=pltpu.SMEM)
BUF = jax.ShapeDtypeStruct((SIDE, PITCH, SIDE), BF16)
NODES = jax.ShapeDtypeStruct((OWN * SIDE, SIDE), BF16)


def fast(source, target, tile_values, tile_rows, tile_peers, need_list, tile_count):
    swap = lambda value: lax.all_to_all(value, "rows", split_axis=0, concat_axis=0, tiled=True)
    buf, slots = pl.pallas_call(
        first_kernel,
        out_shape=(BUF, jax.ShapeDtypeStruct((8, SIDE), jnp.int32)),
        in_specs=[IN_SMEM] * 2 + [IN_VMEM] * 5,
        out_specs=(IN_VMEM, IN_SMEM),
        scratch_shapes=[
            vmem((SIDE * PITCH, SIDE), F32),
            vmem(((CAP + 1) * SIDE, SIDE), F32),
            vmem((8, SIDE), jnp.int32),
            pltpu.SemaphoreType.DMA,
        ],
        compiler_params=pltpu.CompilerParams(vmem_limit_bytes=28 * MIB),
        name="first",
    )(
        tile_count,
        tile_rows,
        tile_peers.reshape(1, SIDE),
        need_list.reshape(1, SIDE),
        tile_values,
        source,
        target,
    )
    recv = swap(buf)
    meta = recv[:, META, :].astype(F32)
    counts = meta[:, CAP].astype(jnp.int32)
    spots = (meta[:, :CAP] * OWN + meta[:, CAP + 1 : 2 * CAP + 1]).astype(jnp.int32)
    index = jnp.pad(spots, ((0, 0), (0, 1)), constant_values=OWN * SIDE)
    carried = jnp.minimum(counts, CAP)
    middle = pl.pallas_call(
        middle_kernel,
        out_shape=BUF,
        in_specs=[IN_SMEM] * 2 + [IN_VMEM],
        out_specs=IN_VMEM,
        scratch_shapes=[
            vmem((OWN * SIDE + 8, SIDE), F32),
            vmem((OWN * SIDE + 8, SIDE), F32),
            vmem((CAP + 1, SIDE), F32),
            vmem((SIDE * (CAP + 1), SIDE), F32),
        ],
        compiler_params=pltpu.CompilerParams(vmem_limit_bytes=28 * MIB),
        name="middle",
    )
    for iteration in range(ITERS):
        recv = swap(middle(index, carried, recv))
        last = iteration == ITERS - 1
        wide = vmem((SIDE * PITCH, SIDE), F32)
        xb = vmem(((CAP + 1) * SIDE, SIDE), BF16)
        acc_x = vmem(((OWN + 1) * SIDE, SIDE), F32)
        acc = vmem(((CAP + 1) * SIDE, SIDE), F32)
        node = vmem((OWN * SIDE, SIDE), BF16)
        out = pl.pallas_call(
            functools.partial(tail_kernel, last),
            out_shape=(NODES, NODES) if last else BUF,
            in_specs=[IN_SMEM] * 3 + [IN_VMEM] * 4,
            out_specs=(IN_VMEM, IN_VMEM) if last else IN_VMEM,
            scratch_shapes=[wide, xb, acc_x] if last else [wide, xb, acc_x, acc, node, node],
            compiler_params=pltpu.CompilerParams(vmem_limit_bytes=32 * MIB),
            name="last" if last else "tail",
        )(tile_count, tile_rows, slots, recv, tile_values, source, target)
        if not last:
            recv = swap(out)
    return out, jnp.max(counts) > CAP


def general(source, target, tile_values, tile_rows, tile_peers, need_list, tile_count):
    peers_total = lax.axis_size("rows")
    row_count = source.shape[0] // SIDE
    tiles_here = tile_values.shape[0]
    group = min(16, tiles_here)
    live = (jnp.arange(tiles_here, dtype=jnp.int32) < tile_count[0]).astype(F32)[:, None, None]
    swap = lambda value: lax.all_to_all(value, "rows", split_axis=0, concat_axis=0, tiled=True)
    send_list = swap(need_list.reshape(peers_total, 1))[:, 0]
    owner_hot = (send_list[None, :] == jnp.arange(row_count, dtype=jnp.int32)[:, None]).astype(F32)

    def take(value, position):
        return lax.dynamic_slice_in_dim(value, position * group, group, 0)

    def product(form, vectors, position, ids):
        return (
            jnp.einsum(form, take(tile_values, position), vectors[ids], preferred_element_type=F32)
            * take(live, position)
        )

    def iterate(_, state):
        source_now, target_now = state
        source_blocks = source_now.reshape(row_count, SIDE, SIDE)
        target_blocks = target_now.reshape(row_count, SIDE, SIDE)

        def backward(position, running):
            part = product("tji,tjk->tik", target_blocks, position, take(tile_rows, position))
            return running.at[take(tile_peers, position)].add(part)

        partial = lax.fori_loop(
            0, tiles_here // group, backward, jnp.zeros((peers_total, SIDE, SIDE), F32)
        )
        both = swap(jnp.stack([source_blocks[send_list], partial.astype(BF16)], axis=1))
        fetched = both[:, 0]

        def forward(position, running):
            part = product("tij,tjk->tik", fetched, position, take(tile_peers, position))
            return running.at[take(tile_rows, position)].add(part)

        gathered = lax.fori_loop(
            0, tiles_here // group, forward, jnp.zeros((row_count, SIDE, SIDE), F32)
        )
        incoming = jnp.dot(
            owner_hot,
            both[:, 1].astype(F32).reshape(peers_total, -1),
            precision=lax.Precision.HIGHEST,
            preferred_element_type=F32,
        )
        return (
            settle(source, gathered.reshape(-1, SIDE)),
            settle(target, incoming.reshape(-1, SIDE)),
        )

    return lax.fori_loop(0, ITERS, iterate, (source, target))


def shards(*args):
    found, over = fast(*args)
    return lax.cond(over, lambda: general(*args), lambda: found)


def solution(mesh):
    return jax.shard_map(
        shards,
        mesh=mesh,
        in_specs=(
            P("rows", None),
            P("rows", None),
            P("rows", None, None),
            P("rows"),
            P("rows"),
            P("rows", None),
            P("rows"),
        ),
        out_specs=(P("rows", None), P("rows", None)),
        check_vma=False,
    )
```

time: 402 us -> 237 us (0.59)
  blocking collectives: 0 us -> 143 us
  other arithmetic: 122 us -> 0.81 us
  local copies, waits for them, and re-layouts: 79.2 us -> 0.11 us
  waiting for transfers between devices: 93.5 us -> 35.3 us
  matrix products: 51.9 us -> 0 us
  Pallas kernels: 0 us -> 49.9 us
  starting transfers between devices: 48.3 us -> 4.66 us
    all_to_all x0 -> x3, blocking collectives: none -> 143 us  [fast(): lax.all_to_all(value, 'rows', split_axis=0, concat_axis=0, tiled=True)]
    scatter-add x32 -> x0, other arithmetic: 78.9 us -> none  [the longest x16 53.2 us: backward_add(): return running.at[peer_ids].add(product)]
    gather x34 -> x0, local copies, waits for them, and re-layouts: 61.8 us -> none  [the longest x16 45.4 us: forward_add(): fetched[peer_ids]]
    all_to_all x5 -> x1, waiting for transfers between devices: 93.5 us -> 35.3 us  [fast(): lax.all_to_all(value, 'rows', split_axis=0, concat_axis=0, tiled=True)]
    dot_general x34 -> x0, matrix products: 51.9 us -> none  [the longest x16 21.4 us: forward_add(): jnp.einsum('tij,tjk->tik', tile_block, fetched[peer_ids], preferred_eleme...]
    pallas_call x0 -> x5, Pallas kernels: none -> 49.9 us  [the longest x2 33.5 us: fast(): recv = swap(middle(index, carried, recv))]
    all_to_all x5 -> x1, starting transfers between devices: 48.3 us -> 4.66 us  [fast(): lax.all_to_all(value, 'rows', split_axis=0, concat_axis=0, tiled=True)]
    convert_element_type x37 -> x2, other arithmetic: 36.8 us -> 0.09 us  [the longest x1 0.08 us: fast(): (meta[:, :CAP] * OWN + meta[:, CAP + 1:2 * CAP + 1]).astype(jnp.int32)]
  transfers between devices with their start and end apart: 5 -> 1, of which waited for: 2 -> 1; matrix products, arithmetic and copies ran while one was open for 49% -> 0% of each run, Pallas kernels for 0% -> 0%
where the time goes in v1:
time: 237 us; the launch traced here: 235 us
  blocking collectives  143 us (60%)
  Pallas kernels  49.9 us (21%)
  waiting for transfers between devices  35.3 us (15%)
  starting transfers between devices  4.66 us (2%)
    all_to_all x3, blocking collectives, fast(): lax.all_to_all(value, 'rows', split_axis=0, concat_axis=0, tiled=True)  143 us
    all_to_all x1, waiting for transfers between devices, fast(): lax.all_to_all(value, 'rows', split_axis=0, concat_axis=0, tiled=True)  35.3 us
    pallas_call x2, Pallas kernels, fast(): recv = swap(middle(index, carried, recv))  33.5 us
    pallas_call x2, Pallas kernels, fast(): pl.pallas_call(functools.partial(tail_kernel, last), out_shape=(NODES, NO...  10.2 us
    pallas_call x1, Pallas kernels, fast(): pl.pallas_call(first_kernel, out_shape=(BUF, jax.ShapeDtypeStruct((8, SID...  6.14 us
  transfers between devices with their start and end apart: 1, of which 1 were waited for; matrix products, arithmetic and copies ran while one was open for 0% of the time, Pallas kernels for 0%

profile of v1, /device:TPU:0, one launch (start us, length us, event | category | flops | bytes accessed | tf_op | source)
XLA Modules:
  0.0 235.4 jit_solution(2788691165587180810)
XLA Ops:
  1.3 6.1 %first.1 = (bf16[128,80,128]{2,1,0:T(8,128)(2,1)S(1)}, s32[8,128]{1,0:T(8,128)S(1)}) custom-call(s32[1]{0:T(128)S(6)} %copy.65.count, s32[128]{0:T(128)} %rows.5, s32[1,128]{1,0:T(1,128)} %bitcast.79, s32[1,128]{1,0:T(1,128)} %need_ref.1, bf16[128,128,128]{2,1,0:T(8,128)(2,1)} %tiles.5, bf16[2048,128]{1,0:T(8,128)(2,1)} %source.3, bf16[2048,128]{1,0:T(8,128)(2,1)} %target.3), custom_call_target="tpu_custom_call" | custom-call | tf_op jit(solution)/shard_map/first/pallas_call | solution.py:218
  7.4 53.4 %all_to_all.35.recv = bf16[128,80,128]{2,1,0:T(8,128)(2,1)S(1)} all-to-all(bf16[128,80,128]{2,1,0:T(8,128)(2,1)S(1)} %get-tuple-element.335), channel_id=1, replica_groups=mesh['rows'=128] {'rows'}, dimensions={0} | all-to-all | bytes 5242880 | tf_op jit(solution)/shard_map/all_to_all | solution.py:217
  60.8 0.1 slice.34
  60.9 0.7 minimum_reduce_fusion
  61.6 0.1 fusion.15
  61.7 0.0 copy-start.1
  61.7 0.0 copy-start.3
  61.7 0.0 copy-start.5
  61.7 0.0 copy-start.7
  61.7 16.0 %middle.2 = bf16[128,80,128]{2,1,0:T(8,128)(2,1)S(1)} custom-call(s32[128,64]{1,0:T(8,128)S(1)} %pad.4.index, s32[128]{0:T(128)S(1)} %get-tuple-element.425.counts, bf16[128,80,128]{2,1,0:T(8,128)(2,1)S(1)} %all_to_all.35.recv), custom_call_target="tpu_custom_call" | custom-call | tf_op jit(solution)/shard_map/middle/pallas_call | solution.py:261
  77.7 40.4 %all_to_all.36.recv = bf16[128,80,128]{2,1,0:T(8,128)(2,1)S(1)} all-to-all(bf16[128,80,128]{2,1,0:T(8,128)(2,1)S(1)} %middle.2), channel_id=1, replica_groups=mesh['rows'=128] {'rows'}, dimensions={0} | all-to-all | bytes 5242880 | tf_op jit(solution)/shard_map/all_to_all | solution.py:217
  118.1 0.0 copy-done.1
  118.1 0.0 copy-done.3
  118.1 0.0 copy-done.5
  118.2 0.0 copy-done.7
  118.2 4.4 %tail.1 = bf16[128,80,128]{2,1,0:T(8,128)(2,1)S(1)} custom-call(s32[1]{0:T(128)S(6)} %copy.65.count, s32[128]{0:T(128)S(1)} %copy-done.7, s32[8,128]{1,0:T(8,128)S(1)} %get-tuple-element.336.slots, bf16[128,80,128]{2,1,0:T(8,128)(2,1)S(1)} %all_to_all.36.recv, bf16[128,128,128]{2,1,0:T(8,128)(2,1)S(1)} %copy-done.1, bf16[2048,128]{1,0:T(8,128)(2,1)S(1)} %copy-done.3, ...), custom_call_target="tpu_custom_call" | custom-call | tf_op jit(solution)/shard_map/tail/pallas_call | solution.py:268
  122.6 48.9 %all_to_all.37.recv = bf16[128,80,128]{2,1,0:T(8,128)(2,1)S(1)} all-to-all(bf16[128,80,128]{2,1,0:T(8,128)(2,1)S(1)} %tail.1), channel_id=1, replica_groups=mesh['rows'=128] {'rows'}, dimensions={0} | all-to-all | bytes 5242880 | tf_op jit(solution)/shard_map/all_to_all | solution.py:217
  171.4 0.0 copy-start.12
  171.4 17.5 %middle.3 = bf16[128,80,128]{2,1,0:T(8,128)(2,1)} custom-call(s32[128,64]{1,0:T(8,128)S(1)} %pad.4.index, s32[128]{0:T(128)S(1)} %get-tuple-element.425.counts, bf16[128,80,128]{2,1,0:T(8,128)(2,1)S(1)} %all_to_all.37.recv), custom_call_target="tpu_custom_call" | custom-call | tf_op jit(solution)/shard_map/middle/pallas_call | solution.py:261
  189.0 4.7 %all-to-all-start.5 = ((bf16[128,80,128]{2,1,0:T(8,128)(2,1)}), bf16[128,80,128]{2,1,0:T(8,128)(2,1)S(1)}, u32[]{:S(2)}, u32[]{:S(2)}) async-start(bf16[128,80,128]{2,1,0:T(8,128)(2,1)} %middle.3), calls=%async_computation.5 | async-start | bytes 5242880 | tf_op jit(solution)/shard_map/all_to_all | solution.py:217
  194.3 35.3 %all-to-all-done.5.recv = bf16[128,80,128]{2,1,0:T(8,128)(2,1)S(1)} async-done(((bf16[128,80,128]{2,1,0:T(8,128)(2,1)}), bf16[128,80,128]{2,1,0:T(8,128)(2,1)S(1)}, u32[]{:S(2)}, u32[]{:S(2)}) %all-to-all-start.5) | async-done | bytes 2621472 | tf_op jit(solution)/shard_map/all_to_all | solution.py:217
  229.6 0.0 copy-done.12
  229.6 5.8 %last.1 = (bf16[2048,128]{1,0:T(8,128)(2,1)}, bf16[2048,128]{1,0:T(8,128)(2,1)}) custom-call(s32[1]{0:T(128)S(6)} %copy.65.count, s32[128]{0:T(128)S(1)} %copy-done.7, s32[8,128]{1,0:T(8,128)S(1)} %get-tuple-element.336.slots, bf16[128,80,128]{2,1,0:T(8,128)(2,1)S(1)} %all-to-all-done.5.recv, bf16[128,128,128]{2,1,0:T(8,128)(2,1)} %tiles.5, ...), custom_call_target="tpu_custom_call" | custom-call | tf_op jit(solution)/shard_map/last/pallas_call | solution.py:268
  (3 shorter events, 0.0 us)
Async XLA Ops:
  61.7 56.4 %copy-start.1 = (bf16[128,128,128]{2,1,0:T(8,128)(2,1)S(1)}, bf16[128,128,128]{2,1,0:T(8,128)(2,1)}, u32[]{:S(2)}) copy-start(bf16[128,128,128]{2,1,0:T(8,128)(2,1)} %tiles.5) | copy-start | bytes 12582916
  61.7 56.4 %copy-start.3 = (bf16[2048,128]{1,0:T(8,128)(2,1)S(1)}, bf16[2048,128]{1,0:T(8,128)(2,1)}, u32[]{:S(2)}) copy-start(bf16[2048,128]{1,0:T(8,128)(2,1)} %source.3) | copy-start | bytes 1572868
  61.7 56.4 %copy-start.5 = (bf16[2048,128]{1,0:T(8,128)(2,1)S(1)}, bf16[2048,128]{1,0:T(8,128)(2,1)}, u32[]{:S(2)}) copy-start(bf16[2048,128]{1,0:T(8,128)(2,1)} %target.3) | copy-start | bytes 1572868
  61.7 56.4 %copy-start.7 = (s32[128]{0:T(128)S(1)}, s32[128]{0:T(128)}, u32[]{:S(2)}) copy-start(s32[128]{0:T(128)} %rows.5) | copy-start | bytes 1540
  171.4 58.2 %copy-start.12 = (s32[1,128]{1,0:T(1,128)S(1)}, s32[1,128]{1,0:T(1,128)}, u32[]{:S(2)}) copy-start(s32[1,128]{1,0:T(1,128)} %need_ref.1) | copy-start | bytes 1540
  189.0 40.6 %all-to-all-start.5 = ((bf16[128,80,128]{2,1,0:T(8,128)(2,1)}), bf16[128,80,128]{2,1,0:T(8,128)(2,1)S(1)}, u32[]{:S(2)}, u32[]{:S(2)}) async-start(bf16[128,80,128]{2,1,0:T(8,128)(2,1)} %middle.3), calls=%async_computation.5 | async-start | bytes 5242880 | tf_op jit(solution)/shard_map/all_to_all | solution.py:217

commit v2 on v1

--- a/solution.py
+++ b/solution.py
@@ -14,6 +14,7 @@
 CAP = 63
 PITCH = OWN + CAP + 1
 META = PITCH - 1
+STRIDE = PITCH + 1
 F32 = jnp.float32
 BF16 = jnp.bfloat16
 MIB = 1 << 20
@@ -31,16 +32,16 @@
 
 def pack_rows(scr, x_ref, acc, peers, buf):
     for b in range(OWN):
-        scr[pl.ds(b, SIDE, stride=PITCH), :] = x_ref[b * SIDE : (b + 1) * SIDE, :].astype(F32)
+        scr[pl.ds(b, SIDE, stride=STRIDE), :] = x_ref[b * SIDE : (b + 1) * SIDE, :].astype(F32)
 
     def put(c, _):
-        scr[pl.ds(OWN + c, SIDE, stride=PITCH), :] = block(acc, c)
+        scr[pl.ds(OWN + c, SIDE, stride=STRIDE), :] = block(acc, c)
         return 0
 
     lax.fori_loop(0, peers, put, 0)
 
     def narrow(i, _):
-        buf[i] = scr[pl.ds(pl.multiple_of(i * PITCH, 8), PITCH), :].astype(BF16)
+        buf[i] = scr[pl.ds(i * STRIDE, PITCH), :].astype(BF16)
         return 0
 
     lax.fori_loop(0, SIDE, narrow, 0, unroll=4)
@@ -58,7 +59,7 @@
     return lax.dot_general(tile, y, (((0,), (0,)), ((), ())), preferred_element_type=F32)
 
 
-STEP = 4
+STEP = 8
 
 
 def first_kernel(
@@ -90,7 +91,7 @@
     pick = (at == (lane_at - CAP - 1).astype(F32)) & (lane_at > CAP)
     need_of = jnp.sum(jnp.where(pick, need_col, 0.0), axis=0, keepdims=True)
     meta = jnp.where(lane < CAP, peer_of, jnp.where(lane == CAP, total, need_of))
-    scr[pl.ds(META, SIDE, stride=PITCH), :] = jnp.broadcast_to(meta, (SIDE, SIDE))
+    scr[pl.ds(META, SIDE, stride=STRIDE), :] = jnp.broadcast_to(meta, (SIDE, SIDE))
     copy.wait()
     peers = slots[1, 0]
     zero(acc, peers)
@@ -109,44 +110,65 @@
     pack_rows(scr, x_ref, acc, peers, buf)
 
 
-LANES8 = 8
-
-
-def middle_kernel(index, counts, recv, buf, xs, acc, parts, outs):
+LOG = CAP.bit_length()
+LIST = SIDE * (CAP + 1) // 8 + 8
+SUMS = OWN * SIDE + 8
+
+
+def middle_kernel(total, batches, index, recv, buf, both, parts, outs):
     def load(d, _):
-        at = pl.ds(pl.multiple_of(d * OWN, OWN), OWN)
-        xs[at, :] = recv[d, 0:OWN, :].astype(F32)
-        acc[at, :] = jnp.zeros((OWN, SIDE), F32)
+        at = pl.multiple_of(d * OWN, OWN)
+        both[pl.ds(at, OWN), :] = recv[d, 0:OWN, :].astype(F32)
+        both[pl.ds(SUMS + at, OWN), :] = jnp.zeros((OWN, SIDE), F32)
         return 0
 
     lax.fori_loop(0, SIDE, load, 0, unroll=4)
-    xs[OWN * SIDE :, :] = jnp.zeros((8, SIDE), F32)
-
-    def reader(d, _):
-        def batch(b, _):
-            start = pl.multiple_of(b * LANES8, LANES8)
-            parts[pl.ds(start, LANES8), :] = recv[d, pl.ds(OWN + start, LANES8), :].astype(F32)
-            spots = [index[d, start + k] for k in range(LANES8)]
-            sums = []
-            for k, spot in enumerate(spots):
-                outs[pl.ds(d * (CAP + 1) + start + k, 1), :] = xs[pl.ds(spot, 1), :]
-                sums.append(acc[pl.ds(spot, 1), :] + parts[pl.ds(start + k, 1), :])
-            for k, spot in enumerate(spots):
-                acc[pl.ds(spot, 1), :] = sums[k]
-            return 0
-
-        lax.fori_loop(0, (counts[d] + LANES8 - 1) // LANES8, batch, 0)
-        return 0
-
-    lax.fori_loop(0, SIDE, reader, 0)
+    both[OWN * SIDE : SUMS, :] = jnp.zeros((8, SIDE), F32)
+
+    def ahead(k):
+        first = pl.multiple_of(batches[k], 8)
+        return first, [index[first + j] for j in range(8)]
+
+    def batch(slot, first, spots):
+        d = jnp.minimum(lax.shift_right_logical(first, LOG), SIDE - 1)
+        start = pl.multiple_of(OWN + (first & CAP), 8)
+        parts[slot : slot + 8, :] = recv[d, pl.ds(start, 8), :].astype(F32)
+        sums = []
+        for j, spot in enumerate(spots):
+            outs[pl.ds(first + j, 1), :] = both[pl.ds(spot, 1), :]
+            sums.append(both[pl.ds(spot + SUMS, 1), :] + parts[slot + j : slot + j + 1, :])
+        for j, spot in enumerate(spots):
+            both[pl.ds(spot + SUMS, 1), :] = sums[j]
+
+    def step(g, now):
+        other = ahead(2 * g + 1)
+        batch(0, *now)
+        later = ahead(2 * g + 2)
+        batch(8, *other)
+        return later
+
+    lax.fori_loop(0, (total[0] + 1) // 2, step, ahead(0))
 
     def narrow(d, _):
-        buf[d, 0:OWN, :] = acc[pl.ds(pl.multiple_of(d * OWN, OWN), OWN), :].astype(BF16)
+        at = pl.multiple_of(SUMS + d * OWN, 8)
+        buf[d, 0:OWN, :] = both[pl.ds(at, OWN), :].astype(BF16)
         at = pl.ds(pl.multiple_of(d * (CAP + 1), CAP + 1), CAP + 1)
         buf[d, OWN:PITCH, :] = outs[at, :].astype(BF16)
         return 0
 
     lax.fori_loop(0, SIDE, narrow, 0, unroll=4)
+
+
+def batch_list(counts):
+    entries = SIDE * (CAP + 1)
+    eights = (counts + 7) // 8
+    order = jnp.arange(SIDE, dtype=jnp.int32)
+    ends = jnp.sum(jnp.where(order[None, :] <= order[:, None], eights[None, :], 0), axis=1)
+    k = jnp.arange(LIST, dtype=jnp.int32)
+    before = ends[None, :] <= k[:, None]
+    device = jnp.sum(before.astype(jnp.int32), axis=1)
+    start = jnp.sum(jnp.where(before, eights[None, :], 0), axis=1)
+    return jnp.minimum(device * (CAP + 1) + (k - start) * 8, entries), ends[-1:]
 
 
 def tail_kernel(
@@ -161,17 +183,17 @@
     peers = slots[1, 0]
 
     def widen(i, _):
-        scr[pl.ds(pl.multiple_of(i * PITCH, 8), PITCH), :] = recv[i].astype(F32)
+        scr[pl.ds(i * STRIDE, PITCH), :] = recv[i].astype(F32)
         return 0
 
     lax.fori_loop(0, SIDE, widen, 0, unroll=4)
     for b in range(OWN):
         at = slice(b * SIDE, (b + 1) * SIDE)
-        y_new[at, :] = settle(target[at, :], scr[pl.ds(b, SIDE, stride=PITCH), :])
+        y_new[at, :] = settle(target[at, :], scr[pl.ds(b, SIDE, stride=STRIDE), :])
 
     def fetch(c, _):
         xb[pl.ds(pl.multiple_of(c * SIDE, SIDE), SIDE), :] = scr[
-            pl.ds(OWN + c, SIDE, stride=PITCH), :
+            pl.ds(OWN + c, SIDE, stride=STRIDE), :
         ].astype(BF16)
         return 0
 
@@ -221,7 +243,7 @@
         in_specs=[IN_SMEM] * 2 + [IN_VMEM] * 5,
         out_specs=(IN_VMEM, IN_SMEM),
         scratch_shapes=[
-            vmem((SIDE * PITCH, SIDE), F32),
+            vmem((SIDE * STRIDE, SIDE), F32),
             vmem(((CAP + 1) * SIDE, SIDE), F32),
             vmem((8, SIDE), jnp.int32),
             pltpu.SemaphoreType.DMA,
@@ -241,26 +263,26 @@
     meta = recv[:, META, :].astype(F32)
     counts = meta[:, CAP].astype(jnp.int32)
     spots = (meta[:, :CAP] * OWN + meta[:, CAP + 1 : 2 * CAP + 1]).astype(jnp.int32)
-    index = jnp.pad(spots, ((0, 0), (0, 1)), constant_values=OWN * SIDE)
-    carried = jnp.minimum(counts, CAP)
+    index = jnp.pad(spots, ((0, 0), (0, 1)), constant_values=OWN * SIDE).reshape(-1)
+    index = jnp.pad(index, (0, 8), constant_values=OWN * SIDE)
+    batches, total = batch_list(jnp.minimum(counts, CAP))
     middle = pl.pallas_call(
         middle_kernel,
         out_shape=BUF,
-        in_specs=[IN_SMEM] * 2 + [IN_VMEM],
+        in_specs=[IN_SMEM] * 3 + [IN_VMEM],
         out_specs=IN_VMEM,
         scratch_shapes=[
-            vmem((OWN * SIDE + 8, SIDE), F32),
-            vmem((OWN * SIDE + 8, SIDE), F32),
-            vmem((CAP + 1, SIDE), F32),
-            vmem((SIDE * (CAP + 1), SIDE), F32),
+            vmem((2 * SUMS, SIDE), F32),
+            vmem((16, SIDE), F32),
+            vmem((SIDE * (CAP + 1) + 8, SIDE), F32),
         ],
         compiler_params=pltpu.CompilerParams(vmem_limit_bytes=28 * MIB),
         name="middle",
     )
     for iteration in range(ITERS):
-        recv = swap(middle(index, carried, recv))
+        recv = swap(middle(total, batches, index, recv))
         last = iteration == ITERS - 1
-        wide = vmem((SIDE * PITCH, SIDE), F32)
+        wide = vmem((SIDE * STRIDE, SIDE), F32)
         xb = vmem(((CAP + 1) * SIDE, SIDE), BF16)
         acc_x = vmem(((OWN + 1) * SIDE, SIDE), F32)
         acc = vmem(((CAP + 1) * SIDE, SIDE), F32)

time: 237 us -> 211 us (0.89)
  blocking collectives: 143 us -> 128 us
  Pallas kernels: 49.9 us -> 39.8 us
    all_to_all x3, blocking collectives: 143 us -> 128 us  [fast(): lax.all_to_all(value, 'rows', split_axis=0, concat_axis=0, tiled=True)]
    pallas_call x2, Pallas kernels: 33.5 us -> 18.7 us  [fast(): recv = swap(middle(total, batches, index, recv))]
    pallas_call x2, Pallas kernels: 10.2 us -> 13.4 us  [fast(): pl.pallas_call(functools.partial(tail_kernel, last), out_shape=(NODES, NO...]
where the time goes in v2:
time: 211 us
  blocking collectives  128 us (61%)
  Pallas kernels  39.8 us (19%)
  waiting for transfers between devices  35.3 us (17%)
  starting transfers between devices  4.66 us (2%)
    all_to_all x3, blocking collectives, fast(): lax.all_to_all(value, 'rows', split_axis=0, concat_axis=0, tiled=True)  128 us
    all_to_all x1, waiting for transfers between devices, fast(): lax.all_to_all(value, 'rows', split_axis=0, concat_axis=0, tiled=True)  35.3 us
    pallas_call x2, Pallas kernels, fast(): recv = swap(middle(total, batches, index, recv))  18.7 us
    pallas_call x2, Pallas kernels, fast(): pl.pallas_call(functools.partial(tail_kernel, last), out_shape=(NODES, NO...  13.4 us
    pallas_call x1, Pallas kernels, fast(): pl.pallas_call(first_kernel, out_shape=(BUF, jax.ShapeDtypeStruct((8, SID...  7.76 us
    all_to_all x1, starting transfers between devices, fast(): lax.all_to_all(value, 'rows', split_axis=0, concat_axis=0, tiled=True)  4.66 us
  transfers between devices with their start and end apart: 1, of which 1 were waited for; matrix products, arithmetic and copies ran while one was open for 0% of the time, Pallas kernels for 0%

profile of v2, /device:TPU:0, one launch (start us, length us, event | category | flops | bytes accessed | tf_op | source)
XLA Modules:
  0.0 211.5 jit_solution(18381864288609674474)
XLA Ops:
  1.3 7.8 %first.1 = (bf16[128,80,128]{2,1,0:T(8,128)(2,1)S(1)}, s32[8,128]{1,0:T(8,128)S(1)}) custom-call(s32[1]{0:T(128)S(6)} %copy.57.count, s32[128]{0:T(128)} %rows.5, s32[1,128]{1,0:T(1,128)} %bitcast.75, s32[1,128]{1,0:T(1,128)} %need_ref.1, bf16[128,128,128]{2,1,0:T(8,128)(2,1)} %tiles.5, bf16[2048,128]{1,0:T(8,128)(2,1)} %source.3, bf16[2048,128]{1,0:T(8,128)(2,1)} %target.3), custom_call_target="tpu_custom_call" | custom-call | tf_op jit(solution)/shard_map/first/pallas_call | solution.py:240
  9.0 46.9 %all_to_all.35.recv = bf16[128,80,128]{2,1,0:T(8,128)(2,1)S(1)} all-to-all(bf16[128,80,128]{2,1,0:T(8,128)(2,1)S(1)} %get-tuple-element.335), channel_id=1, replica_groups=mesh['rows'=128] {'rows'}, dimensions={0} | all-to-all | bytes 5242880 | tf_op jit(solution)/shard_map/all_to_all | solution.py:239
  55.9 0.1 slice_convert_fusion.1
  56.0 0.7 add_reduce_fusion
  56.7 0.1 select_reduce_fusion.1
  56.8 0.4 convert_reduce_fusion
  57.2 0.6 slice.23.total
  57.8 0.1 fusion.15
  57.9 0.1 reshape.117
  58.0 0.0 copy-start.1
  58.0 0.0 copy-start.3
  58.0 0.0 copy-start.5
  58.0 0.0 copy-start.7
  58.0 8.7 %middle.2 = bf16[128,80,128]{2,1,0:T(8,128)(2,1)S(1)} custom-call(s32[1]{0:T(128)} %slice.23.total, s32[1032]{0:T(1024)S(1)} %add_minimum_fusion.batches, s32[8200]{0:T(1024)S(1)} %pad.9.index, bf16[128,80,128]{2,1,0:T(8,128)(2,1)S(1)} %all_to_all.35.recv), custom_call_target="tpu_custom_call" | custom-call | tf_op jit(solution)/shard_map/middle/pallas_call | solution.py:283
  66.7 40.4 %all_to_all.36.recv = bf16[128,80,128]{2,1,0:T(8,128)(2,1)S(1)} all-to-all(bf16[128,80,128]{2,1,0:T(8,128)(2,1)S(1)} %middle.2), channel_id=1, replica_groups=mesh['rows'=128] {'rows'}, dimensions={0} | all-to-all | bytes 5242880 | tf_op jit(solution)/shard_map/all_to_all | solution.py:239
  107.1 0.0 copy-done.1
  107.1 0.0 copy-done.3
  107.1 0.0 copy-done.5
  107.1 0.0 copy-done.7
  107.1 6.3 %tail.1 = bf16[128,80,128]{2,1,0:T(8,128)(2,1)S(1)} custom-call(s32[1]{0:T(128)S(6)} %copy.57.count, s32[128]{0:T(128)S(1)} %copy-done.7, s32[8,128]{1,0:T(8,128)S(1)} %get-tuple-element.336.slots, bf16[128,80,128]{2,1,0:T(8,128)(2,1)S(1)} %all_to_all.36.recv, bf16[128,128,128]{2,1,0:T(8,128)(2,1)S(1)} %copy-done.1, bf16[2048,128]{1,0:T(8,128)(2,1)S(1)} %copy-done.3, ...), custom_call_target="tpu_custom_call" | custom-call | tf_op jit(solution)/shard_map/tail/pallas_call | solution.py:290
  113.4 40.2 %all_to_all.37.recv = bf16[128,80,128]{2,1,0:T(8,128)(2,1)S(1)} all-to-all(bf16[128,80,128]{2,1,0:T(8,128)(2,1)S(1)} %tail.1), channel_id=1, replica_groups=mesh['rows'=128] {'rows'}, dimensions={0} | all-to-all | bytes 5242880 | tf_op jit(solution)/shard_map/all_to_all | solution.py:239
  153.7 0.0 copy-start.12
  153.7 10.0 %middle.3 = bf16[128,80,128]{2,1,0:T(8,128)(2,1)} custom-call(s32[1]{0:T(128)} %slice.23.total, s32[1032]{0:T(1024)S(1)} %add_minimum_fusion.batches, s32[8200]{0:T(1024)S(1)} %pad.9.index, bf16[128,80,128]{2,1,0:T(8,128)(2,1)S(1)} %all_to_all.37.recv), custom_call_target="tpu_custom_call" | custom-call | tf_op jit(solution)/shard_map/middle/pallas_call | solution.py:283
  163.7 4.7 %all-to-all-start.5 = ((bf16[128,80,128]{2,1,0:T(8,128)(2,1)}), bf16[128,80,128]{2,1,0:T(8,128)(2,1)S(1)}, u32[]{:S(2)}, u32[]{:S(2)}) async-start(bf16[128,80,128]{2,1,0:T(8,128)(2,1)} %middle.3), calls=%async_computation.5 | async-start | bytes 5242880 | tf_op jit(solution)/shard_map/all_to_all | solution.py:239
  169.0 35.3 %all-to-all-done.5.recv = bf16[128,80,128]{2,1,0:T(8,128)(2,1)S(1)} async-done(((bf16[128,80,128]{2,1,0:T(8,128)(2,1)}), bf16[128,80,128]{2,1,0:T(8,128)(2,1)S(1)}, u32[]{:S(2)}, u32[]{:S(2)}) %all-to-all-start.5) | async-done | bytes 2621472 | tf_op jit(solution)/shard_map/all_to_all | solution.py:239
  204.3 0.0 copy-done.12
  204.3 7.1 %last.1 = (bf16[2048,128]{1,0:T(8,128)(2,1)}, bf16[2048,128]{1,0:T(8,128)(2,1)}) custom-call(s32[1]{0:T(128)S(6)} %copy.57.count, s32[128]{0:T(128)S(1)} %copy-done.7, s32[8,128]{1,0:T(8,128)S(1)} %get-tuple-element.336.slots, bf16[128,80,128]{2,1,0:T(8,128)(2,1)S(1)} %all-to-all-done.5.recv, bf16[128,128,128]{2,1,0:T(8,128)(2,1)} %tiles.5, ...), custom_call_target="tpu_custom_call" | custom-call | tf_op jit(solution)/shard_map/last/pallas_call | solution.py:290
  (5 shorter events, 0.0 us)
Async XLA Ops:
  58.0 49.1 %copy-start.1 = (bf16[128,128,128]{2,1,0:T(8,128)(2,1)S(1)}, bf16[128,128,128]{2,1,0:T(8,128)(2,1)}, u32[]{:S(2)}) copy-start(bf16[128,128,128]{2,1,0:T(8,128)(2,1)} %tiles.5) | copy-start | bytes 12582916
  58.0 49.1 %copy-start.3 = (bf16[2048,128]{1,0:T(8,128)(2,1)S(1)}, bf16[2048,128]{1,0:T(8,128)(2,1)}, u32[]{:S(2)}) copy-start(bf16[2048,128]{1,0:T(8,128)(2,1)} %source.3) | copy-start | bytes 1572868
  58.0 49.1 %copy-start.5 = (bf16[2048,128]{1,0:T(8,128)(2,1)S(1)}, bf16[2048,128]{1,0:T(8,128)(2,1)}, u32[]{:S(2)}) copy-start(bf16[2048,128]{1,0:T(8,128)(2,1)} %target.3) | copy-start | bytes 1572868
  58.0 49.1 %copy-start.7 = (s32[128]{0:T(128)S(1)}, s32[128]{0:T(128)}, u32[]{:S(2)}) copy-start(s32[128]{0:T(128)} %rows.5) | copy-start | bytes 1540
  153.7 50.7 %copy-start.12 = (s32[1,128]{1,0:T(1,128)S(1)}, s32[1,128]{1,0:T(1,128)}, u32[]{:S(2)}) copy-start(s32[1,128]{1,0:T(1,128)} %need_ref.1) | copy-start | bytes 1540
  163.7 40.6 %all-to-all-start.5 = ((bf16[128,80,128]{2,1,0:T(8,128)(2,1)}), bf16[128,80,128]{2,1,0:T(8,128)(2,1)S(1)}, u32[]{:S(2)}, u32[]{:S(2)}) async-start(bf16[128,80,128]{2,1,0:T(8,128)(2,1)} %middle.3), calls=%async_computation.5 | async-start | bytes 5242880 | tf_op jit(solution)/shard_map/all_to_all | solution.py:239

commit v3 on v2

--- a/solution.py
+++ b/solution.py
@@ -60,11 +60,38 @@
 
 
 STEP = 8
+CHUNK = 16
+
+
+def tile_copy(tiles, held, sems, c):
+    at = pl.ds(pl.multiple_of(c * CHUNK, CHUNK), CHUNK)
+    return pltpu.make_async_copy(tiles.at[at], held.at[at], sems.at[c])
+
+
+def start_tiles(tiles, held, sems):
+    for c in range(SIDE // CHUNK):
+        tile_copy(tiles, held, sems, c).start()
+
+
+def over_tiles(live, step, tiles=None, held=None, sems=None):
+    if tiles is None:
+        lax.fori_loop(0, (live + STEP - 1) // STEP, step, 0)
+        return
+
+    def chunk(c, _):
+        tile_copy(tiles, held, sems, c).wait()
+        first = c * (CHUNK // STEP)
+        end = jnp.minimum((live + STEP - 1) // STEP, first + CHUNK // STEP)
+        lax.fori_loop(first, end, step, 0)
+        return 0
+
+    lax.fori_loop(0, SIDE // CHUNK, chunk, 0)
 
 
 def first_kernel(
-    count, rows, peers_ref, need_ref, tiles, x_ref, y_ref, buf, slots, scr, acc, slot_v, sem
+    count, rows, peers_ref, need_ref, hbm, x_ref, y_ref, buf, slots, scr, acc, slot_v, sem, tiles, sems
 ):
+    start_tiles(hbm, tiles, sems)
     live = count[0]
     row_at = lax.broadcasted_iota(jnp.int32, (SIDE, SIDE), 0)
     lane_at = lax.broadcasted_iota(jnp.int32, (SIDE, SIDE), 1)
@@ -106,77 +133,90 @@
             acc[where, :] = acc[where, :] + part
         return 0
 
-    lax.fori_loop(0, (live + STEP - 1) // STEP, step, 0)
+    over_tiles(live, step, hbm, tiles, sems)
     pack_rows(scr, x_ref, acc, peers, buf)
 
 
 LOG = CAP.bit_length()
 LIST = SIDE * (CAP + 1) // 8 + 8
-SUMS = OWN * SIDE + 8
-
-
-def middle_kernel(total, batches, index, recv, buf, both, parts, outs):
+PAD = 8
+DUMMY = OWN * SIDE
+SUMS = PAD + DUMMY + 16
+
+
+def middle_kernel(batches, index, recv, buf, both):
     def load(d, _):
-        at = pl.multiple_of(d * OWN, OWN)
+        at = pl.multiple_of(PAD + d * OWN, 8)
         both[pl.ds(at, OWN), :] = recv[d, 0:OWN, :].astype(F32)
         both[pl.ds(SUMS + at, OWN), :] = jnp.zeros((OWN, SIDE), F32)
         return 0
 
     lax.fori_loop(0, SIDE, load, 0, unroll=4)
-    both[OWN * SIDE : SUMS, :] = jnp.zeros((8, SIDE), F32)
+    row_at = lax.broadcasted_iota(jnp.int32, (8, SIDE), 0)
+
+    def batch(first, spots):
+        d = lax.shift_right_logical(first, LOG)
+        start = pl.multiple_of(OWN + (first & CAP), 8)
+        parts = recv[d, pl.ds(start, 8), :].astype(F32)
+        picked = both[pl.ds(spots[0] + PAD, 8), :]
+        sums = []
+        for j, spot in enumerate(spots):
+            if j:
+                picked = jnp.where(row_at == j, both[pl.ds(spot + (PAD - j), 8), :], picked)
+            sums.append(both[pl.ds(spot + (SUMS + PAD - j), 8), :] + parts)
+        buf[d, pl.ds(start, 8), :] = picked.astype(BF16)
+        for j, spot in enumerate(spots):
+            window = both.at[pl.ds(spot + (SUMS + PAD - j), 8), :]
+            pltpu.store(window, sums[j], mask=row_at == j)
 
     def ahead(k):
         first = pl.multiple_of(batches[k], 8)
         return first, [index[first + j] for j in range(8)]
 
-    def batch(slot, first, spots):
-        d = jnp.minimum(lax.shift_right_logical(first, LOG), SIDE - 1)
-        start = pl.multiple_of(OWN + (first & CAP), 8)
-        parts[slot : slot + 8, :] = recv[d, pl.ds(start, 8), :].astype(F32)
-        sums = []
-        for j, spot in enumerate(spots):
-            outs[pl.ds(first + j, 1), :] = both[pl.ds(spot, 1), :]
-            sums.append(both[pl.ds(spot + SUMS, 1), :] + parts[slot + j : slot + j + 1, :])
-        for j, spot in enumerate(spots):
-            both[pl.ds(spot + SUMS, 1), :] = sums[j]
-
-    def step(g, now):
-        other = ahead(2 * g + 1)
-        batch(0, *now)
-        later = ahead(2 * g + 2)
-        batch(8, *other)
-        return later
-
-    lax.fori_loop(0, (total[0] + 1) // 2, step, ahead(0))
+    total = batches[LIST - 1]
+
+    def four(g, _):
+        for k in range(4):
+            batch(*ahead(4 * g + k))
+        return 0
+
+    def one(k, _):
+        batch(*ahead(k))
+        return 0
+
+    fours = lax.shift_right_logical(total, 2)
+    lax.fori_loop(0, fours, four, 0)
+    lax.fori_loop(4 * fours, total, one, 0)
 
     def narrow(d, _):
-        at = pl.multiple_of(SUMS + d * OWN, 8)
+        at = pl.multiple_of(SUMS + PAD + d * OWN, 8)
         buf[d, 0:OWN, :] = both[pl.ds(at, OWN), :].astype(BF16)
-        at = pl.ds(pl.multiple_of(d * (CAP + 1), CAP + 1), CAP + 1)
-        buf[d, OWN:PITCH, :] = outs[at, :].astype(BF16)
         return 0
 
     lax.fori_loop(0, SIDE, narrow, 0, unroll=4)
 
 
 def batch_list(counts):
-    entries = SIDE * (CAP + 1)
     eights = (counts + 7) // 8
     order = jnp.arange(SIDE, dtype=jnp.int32)
     ends = jnp.sum(jnp.where(order[None, :] <= order[:, None], eights[None, :], 0), axis=1)
     k = jnp.arange(LIST, dtype=jnp.int32)
+    total = jnp.sum(eights)
     before = ends[None, :] <= k[:, None]
     device = jnp.sum(before.astype(jnp.int32), axis=1)
     start = jnp.sum(jnp.where(before, eights[None, :], 0), axis=1)
-    return jnp.minimum(device * (CAP + 1) + (k - start) * 8, entries), ends[-1:]
+    return jnp.where(k == LIST - 1, total, device * (CAP + 1) + (k - start) * 8)
 
 
 def tail_kernel(
     last, count, rows, slots, recv, tiles, source, target, *rest
 ):
+    coming = ()
     if last:
-        x_new, y_new, scr, xb, acc_x = rest
-        buf = acc = None
+        x_new, y_new, scr, xb, acc_x, held, sems = rest
+        coming = tiles, held, sems
+        start_tiles(*coming)
+        buf, acc, tiles = None, None, held
     else:
         buf, scr, xb, acc_x, acc, x_new, y_new = rest
     live = count[0]
@@ -217,7 +257,7 @@
                 ref[where, :] = ref[where, :] + part
         return 0
 
-    lax.fori_loop(0, (live + STEP - 1) // STEP, step, 0)
+    over_tiles(live, step, *coming)
     for b in range(OWN):
         at = slice(b * SIDE, (b + 1) * SIDE)
         x_new[at, :] = settle(source[at, :], acc_x[at, :])
@@ -231,6 +271,8 @@
 
 IN_VMEM = pl.BlockSpec(memory_space=pltpu.VMEM)
 IN_SMEM = pl.BlockSpec(memory_space=pltpu.SMEM)
+ANYWHERE = pl.BlockSpec(memory_space=pl.ANY)
+TILES_HELD = vmem((SIDE, SIDE, SIDE), BF16), pltpu.SemaphoreType.DMA((SIDE // CHUNK,))
 BUF = jax.ShapeDtypeStruct((SIDE, PITCH, SIDE), BF16)
 NODES = jax.ShapeDtypeStruct((OWN * SIDE, SIDE), BF16)
 
@@ -240,13 +282,14 @@
     buf, slots = pl.pallas_call(
         first_kernel,
         out_shape=(BUF, jax.ShapeDtypeStruct((8, SIDE), jnp.int32)),
-        in_specs=[IN_SMEM] * 2 + [IN_VMEM] * 5,
+        in_specs=[IN_SMEM] * 2 + [IN_VMEM] * 2 + [ANYWHERE] + [IN_VMEM] * 2,
         out_specs=(IN_VMEM, IN_SMEM),
         scratch_shapes=[
             vmem((SIDE * STRIDE, SIDE), F32),
             vmem(((CAP + 1) * SIDE, SIDE), F32),
             vmem((8, SIDE), jnp.int32),
             pltpu.SemaphoreType.DMA,
+            *TILES_HELD,
         ],
         compiler_params=pltpu.CompilerParams(vmem_limit_bytes=28 * MIB),
         name="first",
@@ -263,24 +306,19 @@
     meta = recv[:, META, :].astype(F32)
     counts = meta[:, CAP].astype(jnp.int32)
     spots = (meta[:, :CAP] * OWN + meta[:, CAP + 1 : 2 * CAP + 1]).astype(jnp.int32)
-    index = jnp.pad(spots, ((0, 0), (0, 1)), constant_values=OWN * SIDE).reshape(-1)
-    index = jnp.pad(index, (0, 8), constant_values=OWN * SIDE)
-    batches, total = batch_list(jnp.minimum(counts, CAP))
+    index = jnp.pad(spots, ((0, 0), (0, 1)), constant_values=DUMMY).reshape(-1)
+    batches = batch_list(jnp.minimum(counts, CAP))
     middle = pl.pallas_call(
         middle_kernel,
         out_shape=BUF,
-        in_specs=[IN_SMEM] * 3 + [IN_VMEM],
+        in_specs=[IN_SMEM] * 2 + [IN_VMEM],
         out_specs=IN_VMEM,
-        scratch_shapes=[
-            vmem((2 * SUMS, SIDE), F32),
-            vmem((16, SIDE), F32),
-            vmem((SIDE * (CAP + 1) + 8, SIDE), F32),
-        ],
-        compiler_params=pltpu.CompilerParams(vmem_limit_bytes=28 * MIB),
+        scratch_shapes=[vmem((2 * SUMS, SIDE), F32)],
+        compiler_params=pltpu.CompilerParams(vmem_limit_bytes=16 * MIB),
         name="middle",
     )
     for iteration in range(ITERS):
-        recv = swap(middle(total, batches, index, recv))
+        recv = swap(middle(batches, index, recv))
         last = iteration == ITERS - 1
         wide = vmem((SIDE * STRIDE, SIDE), F32)
         xb = vmem(((CAP + 1) * SIDE, SIDE), BF16)
@@ -290,9 +328,9 @@
         out = pl.pallas_call(
             functools.partial(tail_kernel, last),
             out_shape=(NODES, NODES) if last else BUF,
-            in_specs=[IN_SMEM] * 3 + [IN_VMEM] * 4,
+            in_specs=[IN_SMEM] * 3 + [IN_VMEM, ANYWHERE if last else IN_VMEM] + [IN_VMEM] * 2,
             out_specs=(IN_VMEM, IN_VMEM) if last else IN_VMEM,
-            scratch_shapes=[wide, xb, acc_x] if last else [wide, xb, acc_x, acc, node, node],
+            scratch_shapes=[wide, xb, acc_x, *(TILES_HELD if last else (acc, node, node))],
             compiler_params=pltpu.CompilerParams(vmem_limit_bytes=32 * MIB),
             name="last" if last else "tail",
         )(tile_count, tile_rows, slots, recv, tile_values, source, target)

time: 211 us -> 208 us (0.986)
  Pallas kernels: 39.8 us -> 35.4 us
    pallas_call x2, Pallas kernels: 18.7 us -> 14.6 us  [fast(): recv = swap(middle(batches, index, recv))]
where the time goes in v3:
time: 208 us; the launch traced here: 207 us
  blocking collectives  126 us (61%)
  Pallas kernels  35.4 us (17%)
  waiting for transfers between devices  35.3 us (17%)
  starting transfers between devices  4.66 us (2%)
  other arithmetic  2.65 us (1%)
  between operations  2.23 us (1%)
    all_to_all x3, blocking collectives, fast(): lax.all_to_all(value, 'rows', split_axis=0, concat_axis=0, tiled=True)  126 us
    all_to_all x1, waiting for transfers between devices, fast(): lax.all_to_all(value, 'rows', split_axis=0, concat_axis=0, tiled=True)  35.3 us
    pallas_call x2, Pallas kernels, fast(): recv = swap(middle(batches, index, recv))  14.6 us
    pallas_call x2, Pallas kernels, fast(): pl.pallas_call(functools.partial(tail_kernel, last), out_shape=(NODES, NO...  13.5 us
    pallas_call x1, Pallas kernels, fast(): pl.pallas_call(first_kernel, out_shape=(BUF, jax.ShapeDtypeStruct((8, SID...  7.28 us
    all_to_all x1, starting transfers between devices, fast(): lax.all_to_all(value, 'rows', split_axis=0, concat_axis=0, tiled=True)  4.66 us
  transfers between devices with their start and end apart: 1, of which 1 were waited for; matrix products, arithmetic and copies ran while one was open for 0% of the time, Pallas kernels for 0%

profile of v3, /device:TPU:0, one launch (start us, length us, event | category | flops | bytes accessed | tf_op | source)
XLA Modules:
  0.0 206.9 jit_solution(9553724046424514396)
XLA Ops:
  1.3 7.3 %first.1 = (bf16[128,80,128]{2,1,0:T(8,128)(2,1)S(1)}, s32[8,128]{1,0:T(8,128)S(1)}) custom-call(s32[1]{0:T(128)S(6)} %copy.57.count, s32[128]{0:T(128)} %rows.5, s32[1,128]{1,0:T(1,128)} %bitcast.75, s32[1,128]{1,0:T(1,128)} %need_ref.1, bf16[128,128,128]{2,1,0:T(8,128)(2,1)} %tiles.3, bf16[2048,128]{1,0:T(8,128)(2,1)} %source.3, bf16[2048,128]{1,0:T(8,128)(2,1)} %target.3), custom_call_target="tpu_custom_call" | custom-call | tf_op jit(solution)/shard_map/first/pallas_call | solution.py:282
  8.6 45.9 %all_to_all.35.recv = bf16[128,80,128]{2,1,0:T(8,128)(2,1)S(1)} all-to-all(bf16[128,80,128]{2,1,0:T(8,128)(2,1)S(1)} %get-tuple-element.335), channel_id=1, replica_groups=mesh['rows'=128] {'rows'}, dimensions={0} | all-to-all | bytes 5242880 | tf_op jit(solution)/shard_map/all_to_all | solution.py:281
  54.5 0.1 slice_convert_fusion.1
  54.5 0.7 add_reduce_fusion
  55.3 0.1 fusion.15
  55.4 0.6 fusion.17
  56.0 0.1 select_reduce_fusion.1
  56.1 0.4 convert_reduce_fusion
  56.5 0.1 reshape.117.index
  56.6 0.7 add_select_fusion.batches
  57.3 0.0 copy-start.1
  57.3 0.0 copy-start.3
  57.3 0.0 copy-start.5
  57.3 0.0 copy-start.7
  57.3 6.5 %middle.2 = bf16[128,80,128]{2,1,0:T(8,128)(2,1)S(1)} custom-call(s32[1032]{0:T(1024)S(1)} %add_select_fusion.batches, s32[8192]{0:T(1024)S(1)} %reshape.117.index, bf16[128,80,128]{2,1,0:T(8,128)(2,1)S(1)} %all_to_all.35.recv), custom_call_target="tpu_custom_call" | custom-call | tf_op jit(solution)/shard_map/middle/pallas_call | solution.py:321
  63.8 40.4 %all_to_all.36.recv = bf16[128,80,128]{2,1,0:T(8,128)(2,1)S(1)} all-to-all(bf16[128,80,128]{2,1,0:T(8,128)(2,1)S(1)} %middle.2), channel_id=1, replica_groups=mesh['rows'=128] {'rows'}, dimensions={0} | all-to-all | bytes 5242880 | tf_op jit(solution)/shard_map/all_to_all | solution.py:281
  104.2 0.0 copy-done.1
  104.2 0.0 copy-done.3
  104.2 0.0 copy-done.5
  104.2 0.0 copy-done.7
  104.2 7.0 %tail.1 = bf16[128,80,128]{2,1,0:T(8,128)(2,1)S(1)} custom-call(s32[1]{0:T(128)S(6)} %copy.57.count, s32[128]{0:T(128)S(1)} %copy-done.7, s32[8,128]{1,0:T(8,128)S(1)} %get-tuple-element.336.slots, bf16[128,80,128]{2,1,0:T(8,128)(2,1)S(1)} %all_to_all.36.recv, bf16[128,128,128]{2,1,0:T(8,128)(2,1)S(1)} %copy-done.1, bf16[2048,128]{1,0:T(8,128)(2,1)S(1)} %copy-done.3, ...), custom_call_target="tpu_custom_call" | custom-call | tf_op jit(solution)/shard_map/tail/pallas_call | solution.py:328
  111.2 40.0 %all_to_all.37.recv = bf16[128,80,128]{2,1,0:T(8,128)(2,1)S(1)} all-to-all(bf16[128,80,128]{2,1,0:T(8,128)(2,1)S(1)} %tail.1), channel_id=1, replica_groups=mesh['rows'=128] {'rows'}, dimensions={0} | all-to-all | bytes 5242880 | tf_op jit(solution)/shard_map/all_to_all | solution.py:281
  151.2 0.0 copy-start.12
  151.2 8.1 %middle.3 = bf16[128,80,128]{2,1,0:T(8,128)(2,1)} custom-call(s32[1032]{0:T(1024)S(1)} %add_select_fusion.batches, s32[8192]{0:T(1024)S(1)} %reshape.117.index, bf16[128,80,128]{2,1,0:T(8,128)(2,1)S(1)} %all_to_all.37.recv), custom_call_target="tpu_custom_call" | custom-call | tf_op jit(solution)/shard_map/middle/pallas_call | solution.py:321
  159.3 4.7 %all-to-all-start.5 = ((bf16[128,80,128]{2,1,0:T(8,128)(2,1)}), bf16[128,80,128]{2,1,0:T(8,128)(2,1)S(1)}, u32[]{:S(2)}, u32[]{:S(2)}) async-start(bf16[128,80,128]{2,1,0:T(8,128)(2,1)} %middle.3), calls=%async_computation.5 | async-start | bytes 5242880 | tf_op jit(solution)/shard_map/all_to_all | solution.py:281
  164.6 35.3 %all-to-all-done.5.recv = bf16[128,80,128]{2,1,0:T(8,128)(2,1)S(1)} async-done(((bf16[128,80,128]{2,1,0:T(8,128)(2,1)}), bf16[128,80,128]{2,1,0:T(8,128)(2,1)S(1)}, u32[]{:S(2)}, u32[]{:S(2)}) %all-to-all-start.5) | async-done | bytes 2621472 | tf_op jit(solution)/shard_map/all_to_all | solution.py:281
  199.9 0.0 copy-done.12
  199.9 6.6 %last.1 = (bf16[2048,128]{1,0:T(8,128)(2,1)}, bf16[2048,128]{1,0:T(8,128)(2,1)}) custom-call(s32[1]{0:T(128)S(6)} %copy.57.count, s32[128]{0:T(128)S(1)} %copy-done.7, s32[8,128]{1,0:T(8,128)S(1)} %get-tuple-element.336.slots, bf16[128,80,128]{2,1,0:T(8,128)(2,1)S(1)} %all-to-all-done.5.recv, bf16[128,128,128]{2,1,0:T(8,128)(2,1)} %tiles.3, ...), custom_call_target="tpu_custom_call" | custom-call | tf_op jit(solution)/shard_map/last/pallas_call | solution.py:328
  206.5 0.2 conditional.1
  (1 shorter events, 0.0 us)
Async XLA Ops:
  57.3 47.0 %copy-start.1 = (bf16[128,128,128]{2,1,0:T(8,128)(2,1)S(1)}, bf16[128,128,128]{2,1,0:T(8,128)(2,1)}, u32[]{:S(2)}) copy-start(bf16[128,128,128]{2,1,0:T(8,128)(2,1)} %tiles.3) | copy-start | bytes 12582916
  57.3 47.0 %copy-start.3 = (bf16[2048,128]{1,0:T(8,128)(2,1)S(1)}, bf16[2048,128]{1,0:T(8,128)(2,1)}, u32[]{:S(2)}) copy-start(bf16[2048,128]{1,0:T(8,128)(2,1)} %source.3) | copy-start | bytes 1572868
  57.3 47.0 %copy-start.5 = (bf16[2048,128]{1,0:T(8,128)(2,1)S(1)}, bf16[2048,128]{1,0:T(8,128)(2,1)}, u32[]{:S(2)}) copy-start(bf16[2048,128]{1,0:T(8,128)(2,1)} %target.3) | copy-start | bytes 1572868
  57.3 46.9 %copy-start.7 = (s32[128]{0:T(128)S(1)}, s32[128]{0:T(128)}, u32[]{:S(2)}) copy-start(s32[128]{0:T(128)} %rows.5) | copy-start | bytes 1540
  151.2 48.7 %copy-start.12 = (s32[1,128]{1,0:T(1,128)S(1)}, s32[1,128]{1,0:T(1,128)}, u32[]{:S(2)}) copy-start(s32[1,128]{1,0:T(1,128)} %need_ref.1) | copy-start | bytes 1540
  159.3 40.6 %all-to-all-start.5 = ((bf16[128,80,128]{2,1,0:T(8,128)(2,1)}), bf16[128,80,128]{2,1,0:T(8,128)(2,1)S(1)}, u32[]{:S(2)}, u32[]{:S(2)}) async-start(bf16[128,80,128]{2,1,0:T(8,128)(2,1)} %middle.3), calls=%async_computation.5 | async-start | bytes 5242880 | tf_op jit(solution)/shard_map/all_to_all | solution.py:281

commit v4 on v3

v4 whole, which is shorter than its diff:
```python
import functools
import jax
import jax.numpy as jnp
from jax import lax
from jax.experimental import pallas as pl
from jax.experimental.pallas import tpu as pltpu
from jax.sharding import PartitionSpec as P

ITERS = 2
epsilon = 1e-06

SIDE = 128
OWN = 16
CAP = 63
FEW = 56
PITCH = OWN + CAP + 1
META = PITCH - 1
F32 = jnp.float32
BF16 = jnp.bfloat16
MIB = 1 << 20


def settle(base, update):
    total = base.astype(F32) + update
    scale = lax.rsqrt(jnp.mean(total * total, axis=-1, keepdims=True) + epsilon)
    return (total * scale).astype(BF16)


def block(ref, index):
    return ref[pl.ds(pl.multiple_of(index * SIDE, SIDE), SIDE), :]


def odd_pitch(pitch):
    return pitch + 1


def pack_rows(pitch, scr, x_ref, acc, peers, buf):
    stride = odd_pitch(pitch)
    for b in range(OWN):
        scr[pl.ds(b, SIDE, stride=stride), :] = x_ref[b * SIDE : (b + 1) * SIDE, :].astype(F32)

    def put(c, _):
        scr[pl.ds(OWN + c, SIDE, stride=stride), :] = block(acc, c)
        return 0

    lax.fori_loop(0, peers, put, 0)

    def narrow(i, _):
        buf[i] = scr[pl.ds(i * stride, pitch), :].astype(BF16)
        return 0

    lax.fori_loop(0, SIDE, narrow, 0, unroll=4)


def zero(ref, blocks):
    def one(c, _):
        ref[pl.ds(pl.multiple_of(c * SIDE, SIDE), SIDE), :] = jnp.zeros((SIDE, SIDE), F32)
        return 0

    lax.fori_loop(0, blocks, one, 0)


def back_dot(tile, y):
    return lax.dot_general(tile, y, (((0,), (0,)), ((), ())), preferred_element_type=F32)


STEP = 8
CHUNK = 16


def tile_copy(tiles, held, sems, c):
    at = pl.ds(pl.multiple_of(c * CHUNK, CHUNK), CHUNK)
    return pltpu.make_async_copy(tiles.at[at], held.at[at], sems.at[c])


def start_tiles(tiles, held, sems):
    for c in range(SIDE // CHUNK):
        tile_copy(tiles, held, sems, c).start()


def over_tiles(live, step, tiles=None, held=None, sems=None):
    if tiles is None:
        lax.fori_loop(0, (live + STEP - 1) // STEP, step, 0)
        return

    def chunk(c, _):
        tile_copy(tiles, held, sems, c).wait()
        first = c * (CHUNK // STEP)
        end = jnp.minimum((live + STEP - 1) // STEP, first + CHUNK // STEP)
        lax.fori_loop(first, end, step, 0)
        return 0

    lax.fori_loop(0, SIDE // CHUNK, chunk, 0)


def first_kernel(
    count, rows, peers_ref, need_ref, rows_ref, hbm, source, target, *rest
):
    buf, slots, x_ref, y_ref, scr, acc, slot_v, sem, tiles, sems, node_sems = rest
    y_copy = pltpu.make_async_copy(target, y_ref, node_sems.at[0])
    x_copy = pltpu.make_async_copy(source, x_ref, node_sems.at[1])
    y_copy.start()
    start_tiles(hbm, tiles, sems)
    x_copy.start()
    live = count[0]
    row_at = lax.broadcasted_iota(jnp.int32, (SIDE, SIDE), 0)
    lane_at = lax.broadcasted_iota(jnp.int32, (SIDE, SIDE), 1)
    hit = jnp.where((row_at == peers_ref[...]) & (lane_at < live), 1.0, 0.0)
    used = jnp.broadcast_to(jnp.max(hit, axis=1, keepdims=True), (SIDE, SIDE))
    below = jnp.where(lane_at < row_at, 1.0, 0.0).astype(BF16)
    slot = jnp.dot(below, used.astype(BF16), preferred_element_type=F32)
    total = jnp.sum(used, axis=0, keepdims=True)
    lane = lax.broadcasted_iota(jnp.int32, (1, SIDE), 1)
    mine = jnp.sum(hit * slot, axis=0, keepdims=True)
    mine = jnp.where(lane < live, jnp.minimum(mine, float(CAP)), float(CAP))
    peer_total = jnp.minimum(total, float(CAP))
    slot_v[0:1, :] = mine.astype(jnp.int32)
    slot_v[1:2, :] = peer_total.astype(jnp.int32)
    slot_v[2:3, :] = rows_ref[...]
    slot_v[3:4, :] = jnp.zeros((1, SIDE), jnp.int32) + live
    copy = pltpu.make_async_copy(slot_v, slots, sem)
    copy.start()
    order = lane_at & CAP
    order = ((order & 7) * 8 + lax.shift_right_logical(order, 3)).astype(F32)
    pick = (used > 0) & (slot == order)
    peer_of = jnp.sum(jnp.where(pick, row_at.astype(F32), 0.0), axis=0, keepdims=True)
    peer_of = jnp.where(order[0:1, :] < total, peer_of, float(SIDE))
    need_col = jnp.sum(
        jnp.where(row_at == lane_at, need_ref[...], 0).astype(F32), axis=1, keepdims=True
    )
    need_of = jnp.sum(jnp.where(pick, need_col, 0.0), axis=0, keepdims=True)
    meta = jnp.where(lane < CAP, peer_of, jnp.where(lane == CAP, total, need_of))
    scr[pl.ds(META, SIDE, stride=odd_pitch(PITCH)), :] = jnp.broadcast_to(meta, (SIDE, SIDE))
    copy.wait()
    peers = slots[1, 0]
    zero(acc, peers)
    y_copy.wait()

    def step(g, _):
        parts = []
        for k in range(STEP):
            t = g * STEP + k
            parts.append((slots[0, t], back_dot(tiles[t], block(y_ref, rows[t]))))
        for s, part in parts:
            where = pl.ds(pl.multiple_of(s * SIDE, SIDE), SIDE)
            acc[where, :] = acc[where, :] + part
        return 0

    over_tiles(live, step, hbm, tiles, sems)
    x_copy.wait()
    pack_rows(PITCH, scr, x_ref, acc, peers, buf)


GROUPS = SIDE * (CAP + 1) // 8
PAD = 8
DUMMY = OWN * SIDE
SUMS = PAD + DUMMY + 16


def middle_kernel(*refs):
    *index, onward, recv, buf, even, odd = refs

    def load(d, _):
        at = pl.multiple_of(PAD + d * OWN, 8)
        rows = recv[d, 0:OWN, :].astype(F32)
        for ref in (even, odd):
            ref[pl.ds(at, OWN), :] = rows
            ref[pl.ds(SUMS + at, OWN), :] = jnp.zeros((OWN, SIDE), F32)
        return 0

    lax.fori_loop(0, SIDE, load, 0, unroll=4)
    row_at = lax.broadcasted_iota(jnp.int32, (8, SIDE), 0)

    def clip(group):
        return jnp.where(group < GROUPS, group, GROUPS - 8)

    def after(group):
        return group + onward[clip(group)]

    def work(groups):
        jobs = []
        for ref, group in zip((even, odd), groups):
            spots = [entry[clip(group)] for entry in index]
            d = lax.shift_right_logical(clip(group), 3)
            at = d, pl.ds(pl.multiple_of(OWN + (clip(group) & 7) * 8, 8), 8), slice(None)
            parts = jnp.where(group >= GROUPS, 0.0, recv[at].astype(F32))
            jobs.append((ref, spots, at, parts))
        found = []
        for ref, spots, at, parts in jobs:
            picked = ref[pl.ds(spots[0] + PAD, 8), :]
            sums = [ref[pl.ds(spots[0] + SUMS + PAD, 8), :] + parts]
            for j in range(1, 8):
                picked = jnp.where(row_at == j, ref[pl.ds(spots[j] + PAD - j, 8), :], picked)
                sums.append(ref[pl.ds(spots[j] + (SUMS + PAD - j), 8), :] + parts)
            found.append((picked, sums))
        for (ref, spots, at, _), (picked, sums) in zip(jobs, found):
            buf[at] = picked.astype(BF16)
            for j, spot in enumerate(spots):
                window = ref.at[pl.ds(spot + (SUMS + PAD - j), 8), :]
                pltpu.store(window, sums[j], mask=row_at == j)

    def two(groups):
        first = after(groups[1])
        second = after(first)
        third = after(second)
        fourth = after(third)
        work(groups)
        work((first, second))
        return third, fourth

    lax.while_loop(lambda groups: groups[0] < GROUPS, two, (jnp.int32(0), after(jnp.int32(0))))

    def narrow(d, _):
        at = pl.ds(pl.multiple_of(SUMS + PAD + d * OWN, 8), OWN)
        buf[d, 0:OWN, :] = (even[at, :] + odd[at, :]).astype(BF16)
        return 0

    lax.fori_loop(0, SIDE, narrow, 0, unroll=4)


def tail_kernel(
    last, pitch, slots, recv, tiles, source, target, *rest
):
    if last:
        x_new, y_new, scr, xb, acc_x = rest
        buf = acc = None
    else:
        buf, scr, xb, acc_x, acc, x_new, y_new = rest
    live = slots[3, 0]
    peers = slots[1, 0]
    stride = odd_pitch(pitch)

    def widen(i, _):
        scr[pl.ds(i * stride, pitch), :] = recv[i].astype(F32)
        return 0

    lax.fori_loop(0, SIDE, widen, 0, unroll=4)
    for b in range(OWN):
        at = slice(b * SIDE, (b + 1) * SIDE)
        y_new[at, :] = settle(target[at, :], scr[pl.ds(b, SIDE, stride=stride), :])

    def fetch(c, _):
        xb[pl.ds(pl.multiple_of(c * SIDE, SIDE), SIDE), :] = scr[
            pl.ds(OWN + c, SIDE, stride=stride), :
        ].astype(BF16)
        return 0

    lax.fori_loop(0, peers, fetch, 0)
    zero(acc_x, OWN)
    if not last:
        zero(acc, peers)

    def step(g, _):
        ahead, back = [], []
        for k in range(STEP):
            t = g * STEP + k
            s, r, tile = slots[0, t], slots[2, t], tiles[t]
            to = jnp.where(t < live, r, OWN)
            ahead.append((to, jnp.dot(tile, block(xb, s), preferred_element_type=F32)))
            if not last:
                back.append((s, back_dot(tile, block(y_new, r))))
        for ref, found in ((acc_x, ahead), (acc, back)):
            for s, part in found:
                where = pl.ds(pl.multiple_of(s * SIDE, SIDE), SIDE)
                ref[where, :] = ref[where, :] + part
        return 0

    over_tiles(live, step)
    for b in range(OWN):
        at = slice(b * SIDE, (b + 1) * SIDE)
        x_new[at, :] = settle(source[at, :], acc_x[at, :])
    if not last:
        pack_rows(pitch, scr, x_new, acc, peers, buf)


def vmem(shape, dtype):
    return pltpu.VMEM(shape, dtype)


IN_VMEM = pl.BlockSpec(memory_space=pltpu.VMEM)
IN_SMEM = pl.BlockSpec(memory_space=pltpu.SMEM)
ANYWHERE = pl.BlockSpec(memory_space=pl.ANY)
NODES = jax.ShapeDtypeStruct((OWN * SIDE, SIDE), BF16)


def buffer(pitch):
    return jax.ShapeDtypeStruct((SIDE, pitch, SIDE), BF16)


def wide(pitch):
    return vmem((SIDE * odd_pitch(pitch), SIDE), F32)


def swap(value):
    return lax.all_to_all(value, "rows", split_axis=0, concat_axis=0, tiled=True)


def begin(source, target, tile_values, tile_rows, tile_peers, need_list, tile_count):
    buf, slots, *kept = pl.pallas_call(
        first_kernel,
        out_shape=(buffer(PITCH), jax.ShapeDtypeStruct((8, SIDE), jnp.int32), NODES, NODES),
        in_specs=[IN_SMEM] * 2 + [IN_VMEM] * 3 + [ANYWHERE] * 3,
        out_specs=(IN_VMEM, IN_SMEM, IN_VMEM, IN_VMEM),
        scratch_shapes=[
            wide(PITCH),
            vmem(((CAP + 1) * SIDE, SIDE), F32),
            vmem((8, SIDE), jnp.int32),
            pltpu.SemaphoreType.DMA,
            vmem((SIDE, SIDE, SIDE), BF16),
            pltpu.SemaphoreType.DMA((SIDE // CHUNK,)),
            pltpu.SemaphoreType.DMA((2,)),
        ],
        compiler_params=pltpu.CompilerParams(vmem_limit_bytes=28 * MIB),
        name="first",
    )(
        tile_count,
        tile_rows,
        tile_peers.reshape(1, SIDE),
        need_list.reshape(1, SIDE),
        tile_rows.reshape(1, SIDE),
        tile_values,
        source,
        target,
    )
    recv = swap(buf)
    meta = recv[:, META, :].astype(F32)
    most = jnp.max(meta[:, CAP])
    which = (most > FEW).astype(jnp.int32) + (most > CAP).astype(jnp.int32)
    return recv, meta, slots, kept, which, most


def proceed(pitch, recv, meta, slots, source, target, tile_values):
    lane = lax.broadcasted_iota(jnp.int32, (SIDE, CAP + 1), 1)
    spots = meta[:, : CAP + 1] * OWN + meta[:, CAP + 1 :]
    spots = jnp.where(lane == CAP, float(DUMMY), spots)
    peers = jnp.minimum(meta[:, CAP : CAP + 1], float(CAP))
    spots = spots.astype(jnp.int32)
    index = [spots[:, 8 * j : 8 * j + 8].reshape(-1) for j in range(8)]
    place = lax.broadcasted_iota(jnp.int32, (SIDE, 8), 1)
    index.append(jnp.where((8 * place + 8).astype(F32) < peers, 1, 8 - place).reshape(-1))
    middle = pl.pallas_call(
        middle_kernel,
        out_shape=buffer(pitch),
        in_specs=[IN_SMEM] * 9 + [IN_VMEM],
        out_specs=IN_VMEM,
        scratch_shapes=[vmem((2 * SUMS, SIDE), F32)] * 2,
        compiler_params=pltpu.CompilerParams(vmem_limit_bytes=16 * MIB),
        name="middle",
    )
    xb = vmem(((CAP + 1) * SIDE, SIDE), BF16)
    acc_x = vmem(((OWN + 1) * SIDE, SIDE), F32)
    acc = vmem(((CAP + 1) * SIDE, SIDE), F32)
    node = vmem((OWN * SIDE, SIDE), BF16)
    for iteration in range(ITERS):
        recv = swap(middle(*index, recv))
        last = iteration == ITERS - 1
        out = pl.pallas_call(
            functools.partial(tail_kernel, last, pitch),
            out_shape=(NODES, NODES) if last else buffer(pitch),
            in_specs=[IN_SMEM] + [IN_VMEM] * 4,
            out_specs=(IN_VMEM, IN_VMEM) if last else IN_VMEM,
            scratch_shapes=[wide(pitch), xb, acc_x, *(() if last else (acc, node, node))],
            compiler_params=pltpu.CompilerParams(vmem_limit_bytes=32 * MIB),
            name="last" if last else "tail",
        )(slots, recv, tile_values, source, target)
        if not last:
            recv = swap(out)
    return out


def general(source, target, tile_values, tile_rows, tile_peers, need_list, tile_count):
    peers_total = lax.axis_size("rows")
    row_count = source.shape[0] // SIDE
    tiles_here = tile_values.shape[0]
    group = min(16, tiles_here)
    live = (jnp.arange(tiles_here, dtype=jnp.int32) < tile_count[0]).astype(F32)[:, None, None]
    send_list = swap(need_list.reshape(peers_total, 1))[:, 0]
    owner_hot = (send_list[None, :] == jnp.arange(row_count, dtype=jnp.int32)[:, None]).astype(F32)

    def take(value, position):
        return lax.dynamic_slice_in_dim(value, position * group, group, 0)

    def product(form, vectors, position, ids):
        return (
            jnp.einsum(form, take(tile_values, position), vectors[ids], preferred_element_type=F32)
            * take(live, position)
        )

    def iterate(_, state):
        source_now, target_now = state
        source_blocks = source_now.reshape(row_count, SIDE, SIDE)
        target_blocks = target_now.reshape(row_count, SIDE, SIDE)

        def backward(position, running):
            part = product("tji,tjk->tik", target_blocks, position, take(tile_rows, position))
            return running.at[take(tile_peers, position)].add(part)

        partial = lax.fori_loop(
            0, tiles_here // group, backward, jnp.zeros((peers_total, SIDE, SIDE), F32)
        )
        both = swap(jnp.stack([source_blocks[send_list], partial.astype(BF16)], axis=1))
        fetched = both[:, 0]

        def forward(position, running):
            part = product("tij,tjk->tik", fetched, position, take(tile_peers, position))
            return running.at[take(tile_rows, position)].add(part)

        gathered = lax.fori_loop(
            0, tiles_here // group, forward, jnp.zeros((row_count, SIDE, SIDE), F32)
        )
        incoming = jnp.dot(
            owner_hot,
            both[:, 1].astype(F32).reshape(peers_total, -1),
            precision=lax.Precision.HIGHEST,
            preferred_element_type=F32,
        )
        return (
            settle(source, gathered.reshape(-1, SIDE)),
            settle(target, incoming.reshape(-1, SIDE)),
        )

    return lax.fori_loop(0, ITERS, iterate, (source, target))


def shards(*args):
    recv, meta, slots, nodes, which, most = begin(*args)
    onward = recv, meta, slots, *nodes, args[2]
    return lax.switch(
        which,
        [
            lambda: proceed(OWN + FEW, *onward),
            lambda: proceed(PITCH, *onward),
            lambda: general(*args[:6], jnp.where(most > 0, args[6], 0)),
        ],
    )


def solution(mesh):
    return jax.shard_map(
        shards,
        mesh=mesh,
        in_specs=(
            P("rows", None),
            P("rows", None),
            P("rows", None, None),
            P("rows"),
            P("rows"),
            P("rows", None),
            P("rows"),
        ),
        out_specs=(P("rows", None), P("rows", None)),
        check_vma=False,
    )
```

time: 208 us -> 199 us (0.957); the launches traced: 207 us -> 202 us
  blocking collectives: 126 us -> 172 us
  waiting for transfers between devices: 35.3 us -> 0 us
  Pallas kernels: 35.4 us -> 24.4 us
  starting transfers between devices: 4.66 us -> 0 us
    all_to_all x3 -> x4, blocking collectives: 126 us -> 172 us  [swap(): lax.all_to_all(value, 'rows', split_axis=0, concat_axis=0, tiled=True)]
    all_to_all x1 -> x0, waiting for transfers between devices: 35.3 us -> none  [fast(): lax.all_to_all(value, 'rows', split_axis=0, concat_axis=0, tiled=True)]
    pallas_call x5, Pallas kernels: 35.4 us -> 24.4 us  [the longest x2 12.2 us: proceed(): recv = swap(middle(*index, recv))]
    all_to_all x1 -> x0, starting transfers between devices: 4.66 us -> none  [fast(): lax.all_to_all(value, 'rows', split_axis=0, concat_axis=0, tiled=True)]
  transfers between devices with their start and end apart: 1 -> 0, of which waited for: 1 -> 0; matrix products, arithmetic and copies ran while one was open for 0% -> 0% of each run, Pallas kernels for 0% -> 0%
where the time goes in v4:
time: 199 us; the launch traced here: 202 us
  blocking collectives  172 us (86%)
  Pallas kernels  24.4 us (12%)
  between operations  2.58 us (1%)
    all_to_all x4, blocking collectives, swap(): lax.all_to_all(value, 'rows', split_axis=0, concat_axis=0, tiled=True)  172 us
    pallas_call x2, Pallas kernels, proceed(): recv = swap(middle(*index, recv))  12.2 us
    pallas_call x2, Pallas kernels, proceed(): pl.pallas_call(functools.partial(tail_kernel, last, pitch), out_shape=(NO...  7.02 us
    pallas_call x1, Pallas kernels, begin(): pl.pallas_call(first_kernel, out_shape=(buffer(PITCH), jax.ShapeDtypeStru...  5.23 us

profile of v4, /device:TPU:0, one launch (start us, length us, event | category | flops | bytes accessed | tf_op | source)
XLA Modules:
  0.0 202.0 jit_solution(5897266981036788441)
XLA Ops:
  1.3 5.2 %first.1 = (bf16[128,80,128]{2,1,0:T(8,128)(2,1)S(1)}, s32[8,128]{1,0:T(8,128)S(1)}, bf16[2048,128]{1,0:T(8,128)(2,1)S(1)}, bf16[2048,128]{1,0:T(8,128)(2,1)}) custom-call(s32[1]{0:T(128)S(6)} %copy.115.count, s32[128]{0:T(128)} %rows.1, s32[1,128]{1,0:T(1,128)} %bitcast.79, s32[1,128]{1,0:T(1,128)} %need_ref.1, s32[1,128]{1,0:T(1,128)} %bitcast.78, ...), custom_call_target="tpu_custom_call" | custom-call | tf_op jit(solution)/shard_map/first/pallas_call | solution.py:299
  6.5 49.0 %all_to_all.50 = bf16[128,80,128]{2,1,0:T(8,128)(2,1)S(1)} all-to-all(bf16[128,80,128]{2,1,0:T(8,128)(2,1)S(1)} %get-tuple-element.372), channel_id=1, replica_groups=mesh['rows'=128] {'rows'}, dimensions={0} | all-to-all | bytes 5242880 | tf_op jit(solution)/shard_map/all_to_all | solution.py:295
  55.6 0.1 slice_convert_fusion
  55.6 0.7 slice_reduce_fusion
  57.6 144.4 %conditional.1 = ((bf16[2048,128]{1,0:T(8,128)(2,1)}, bf16[2048,128]{1,0:T(8,128)(2,1)})) conditional(s32[]{:T(128)} %clamp.3, (f32[128,128]{1,0:T(8,128)S(1)}, bf16[128,80,128]{2,1,0:T(8,128)(2,1)S(1)}, s32[8,128]{1,0:T(8,128)S(1)}, bf16[128,128,128]{2,1,0:T(8,128)(2,1)}, bf16[2048,128]{1,0:T(8,128)(2,1)S(1)}, ...), branch_computations={%region_1.2_spmd, %region_2.3_spmd, %region_3.14_spmd} | conditional | flops 548417344 | bytes 118714216 | solution.py:428
  57.7 0.1 copy.76
  57.8 0.1 fusion.8
  57.9 0.1 copy.65
  58.0 0.1 reshape.141.refs_0_
  58.1 0.1 copy.66
  58.2 0.1 reshape.142.refs_1_
  58.3 0.1 copy.67
  58.4 0.1 reshape.143.refs_2_
  58.5 0.1 copy.68
  58.6 0.1 reshape.144.refs_3_
  58.7 0.1 copy.69
  58.8 0.1 reshape.145.refs_4_
  58.9 0.1 copy.70
  59.0 0.1 reshape.146.refs_5_
  59.0 0.1 copy.71
  59.1 0.1 reshape.147.refs_6_
  59.2 0.1 copy.72
  59.3 0.1 reshape.148.refs_7_
  59.4 0.1 compare_select_fusion.1
  59.5 0.1 select_n.78.refs_8_
  59.6 6.1 %middle.6 = bf16[128,80,128]{2,1,0:T(8,128)(2,1)S(1)} custom-call(s32[1024]{0:T(1024)S(1)} %reshape.141.refs_0_, s32[1024]{0:T(1024)S(1)} %reshape.142.refs_1_, s32[1024]{0:T(1024)S(1)} %reshape.143.refs_2_, s32[1024]{0:T(1024)S(1)} %reshape.144.refs_3_, s32[1024]{0:T(1024)S(1)} %reshape.145.refs_4_, s32[1024]{0:T(1024)S(1)} %reshape.146.refs_5_, ...), custom_call_target="tpu_custom_call" | custom-call | tf_op jit(solution)/shard_map/cond/branch_1_fun/middle/pallas_call | solution.py:355
  65.7 40.4 %all_to_all.47.recv = bf16[128,80,128]{2,1,0:T(8,128)(2,1)S(1)} all-to-all(bf16[128,80,128]{2,1,0:T(8,128)(2,1)S(1)} %middle.6), channel_id=1, replica_groups=mesh['rows'=128] {'rows'}, dimensions={0} | all-to-all | bytes 5242880 | tf_op jit(solution)/shard_map/cond/branch_1_fun/all_to_all | solution.py:295
  106.1 3.5 %tail.3 = bf16[128,80,128]{2,1,0:T(8,128)(2,1)S(1)} custom-call(s32[8,128]{1,0:T(8,128)S(1)} %get-tuple-element.320.slots, bf16[128,80,128]{2,1,0:T(8,128)(2,1)S(1)} %all_to_all.47.recv, bf16[128,128,128]{2,1,0:T(8,128)(2,1)S(1)} %copy-done.1, bf16[2048,128]{1,0:T(8,128)(2,1)S(1)} %get-tuple-element.324.source, bf16[2048,128]{1,0:T(8,128)(2,1)S(1)} %copy-done.3), custom_call_target="tpu_custom_call" | custom-call | tf_op jit(solution)/shard_map/cond/branch_1_fun/tail/pallas_call | solution.py:357
  109.6 42.4 %all_to_all.48.refs_9_ = bf16[128,80,128]{2,1,0:T(8,128)(2,1)S(1)} all-to-all(bf16[128,80,128]{2,1,0:T(8,128)(2,1)S(1)} %tail.3), channel_id=1, replica_groups=mesh['rows'=128] {'rows'}, dimensions={0} | all-to-all | bytes 5242880 | tf_op jit(solution)/shard_map/cond/branch_1_fun/all_to_all | solution.py:295
  152.0 6.1 %middle.7 = bf16[128,80,128]{2,1,0:T(8,128)(2,1)S(1)} custom-call(s32[1024]{0:T(1024)S(1)} %reshape.141.refs_0_, s32[1024]{0:T(1024)S(1)} %reshape.142.refs_1_, s32[1024]{0:T(1024)S(1)} %reshape.143.refs_2_, s32[1024]{0:T(1024)S(1)} %reshape.144.refs_3_, s32[1024]{0:T(1024)S(1)} %reshape.145.refs_4_, s32[1024]{0:T(1024)S(1)} %reshape.146.refs_5_, ...), custom_call_target="tpu_custom_call" | custom-call | tf_op jit(solution)/shard_map/cond/branch_1_fun/middle/pallas_call | solution.py:355
  158.1 40.4 %all_to_all.49.recv = bf16[128,80,128]{2,1,0:T(8,128)(2,1)S(1)} all-to-all(bf16[128,80,128]{2,1,0:T(8,128)(2,1)S(1)} %middle.7), channel_id=1, replica_groups=mesh['rows'=128] {'rows'}, dimensions={0} | all-to-all | bytes 5242880 | tf_op jit(solution)/shard_map/cond/branch_1_fun/all_to_all | solution.py:295
  198.5 3.5 %last.3 = (bf16[2048,128]{1,0:T(8,128)(2,1)}, bf16[2048,128]{1,0:T(8,128)(2,1)}) custom-call(s32[8,128]{1,0:T(8,128)S(1)} %get-tuple-element.320.slots, bf16[128,80,128]{2,1,0:T(8,128)(2,1)S(1)} %all_to_all.49.recv, bf16[128,128,128]{2,1,0:T(8,128)(2,1)S(1)} %copy-done.1, bf16[2048,128]{1,0:T(8,128)(2,1)S(1)} %get-tuple-element.324.source, ...), custom_call_target="tpu_custom_call" | custom-call | tf_op jit(solution)/shard_map/cond/branch_1_fun/last/pallas_call | solution.py:357
  (10 shorter events, 0.0 us)
Async XLA Ops:
  1.3 56.3 %copy-start.8 = (s32[1,128]{1,0:T(1,128)S(1)}, s32[1,128]{1,0:T(1,128)}, u32[]{:S(2)}) copy-start(s32[1,128]{1,0:T(1,128)} %need_ref.1) | copy-start | bytes 1540
  59.6 46.5 %copy-start.1 = (bf16[128,128,128]{2,1,0:T(8,128)(2,1)S(1)}, bf16[128,128,128]{2,1,0:T(8,128)(2,1)}, u32[]{:S(2)}) copy-start(bf16[128,128,128]{2,1,0:T(8,128)(2,1)} %get-tuple-element.323.tiles) | copy-start | bytes 12582916 | tf_op jit(solution)/shard_map/cond
  59.6 46.5 %copy-start.3 = (bf16[2048,128]{1,0:T(8,128)(2,1)S(1)}, bf16[2048,128]{1,0:T(8,128)(2,1)}, u32[]{:S(2)}) copy-start(bf16[2048,128]{1,0:T(8,128)(2,1)} %get-tuple-element.325.target) | copy-start | bytes 1572868 | tf_op jit(solution)/shard_map/cond

commit v5 on v4

--- a/solution.py
+++ b/solution.py
@@ -94,14 +94,12 @@
 
 
 def first_kernel(
-    count, rows, peers_ref, need_ref, rows_ref, hbm, source, target, *rest
+    count, rows, peers_ref, need_ref, rows_ref, hbm, x_ref, y_ref, *rest
 ):
-    buf, slots, x_ref, y_ref, scr, acc, slot_v, sem, tiles, sems, node_sems = rest
-    y_copy = pltpu.make_async_copy(target, y_ref, node_sems.at[0])
-    x_copy = pltpu.make_async_copy(source, x_ref, node_sems.at[1])
-    y_copy.start()
+    buf, slots, x_kept, y_kept, scr, acc, slot_v, sem, tiles, sems = rest
     start_tiles(hbm, tiles, sems)
-    x_copy.start()
+    x_kept[...] = x_ref[...]
+    y_kept[...] = y_ref[...]
     live = count[0]
     row_at = lax.broadcasted_iota(jnp.int32, (SIDE, SIDE), 0)
     lane_at = lax.broadcasted_iota(jnp.int32, (SIDE, SIDE), 1)
@@ -129,12 +127,13 @@
         jnp.where(row_at == lane_at, need_ref[...], 0).astype(F32), axis=1, keepdims=True
     )
     need_of = jnp.sum(jnp.where(pick, need_col, 0.0), axis=0, keepdims=True)
+    kind = jnp.where(total > FEW, 1.0, 0.0) + jnp.where(total > CAP, 1.0, 0.0)
     meta = jnp.where(lane < CAP, peer_of, jnp.where(lane == CAP, total, need_of))
+    meta = jnp.where(lane == SIDE - 1, kind, meta)
     scr[pl.ds(META, SIDE, stride=odd_pitch(PITCH)), :] = jnp.broadcast_to(meta, (SIDE, SIDE))
     copy.wait()
     peers = slots[1, 0]
     zero(acc, peers)
-    y_copy.wait()
 
     def step(g, _):
         parts = []
@@ -147,7 +146,6 @@
         return 0
 
     over_tiles(live, step, hbm, tiles, sems)
-    x_copy.wait()
     pack_rows(PITCH, scr, x_ref, acc, peers, buf)
 
 
@@ -172,17 +170,14 @@
     row_at = lax.broadcasted_iota(jnp.int32, (8, SIDE), 0)
 
     def clip(group):
-        return jnp.where(group < GROUPS, group, GROUPS - 8)
-
-    def after(group):
-        return group + onward[clip(group)]
+        return jnp.where(group < GROUPS, group, SIDE - 1)
 
     def work(groups):
         jobs = []
         for ref, group in zip((even, odd), groups):
             spots = [entry[clip(group)] for entry in index]
-            d = lax.shift_right_logical(clip(group), 3)
-            at = d, pl.ds(pl.multiple_of(OWN + (clip(group) & 7) * 8, 8), 8), slice(None)
+            start = OWN + lax.shift_right_logical(clip(group), 7) * 8
+            at = clip(group) & (SIDE - 1), pl.ds(pl.multiple_of(start, 8), 8), slice(None)
             parts = jnp.where(group >= GROUPS, 0.0, recv[at].astype(F32))
             jobs.append((ref, spots, at, parts))
         found = []
@@ -200,15 +195,15 @@
                 pltpu.store(window, sums[j], mask=row_at == j)
 
     def two(groups):
-        first = after(groups[1])
-        second = after(first)
-        third = after(second)
-        fourth = after(third)
+        first = onward[groups[1]]
+        second = onward[first]
+        third = onward[second]
+        fourth = onward[third]
         work(groups)
         work((first, second))
         return third, fourth
 
-    lax.while_loop(lambda groups: groups[0] < GROUPS, two, (jnp.int32(0), after(jnp.int32(0))))
+    lax.while_loop(lambda groups: groups[0] < GROUPS, two, (jnp.int32(0), onward[0]))
 
     def narrow(d, _):
         at = pl.ds(pl.multiple_of(SUMS + PAD + d * OWN, 8), OWN)
@@ -299,7 +294,7 @@
     buf, slots, *kept = pl.pallas_call(
         first_kernel,
         out_shape=(buffer(PITCH), jax.ShapeDtypeStruct((8, SIDE), jnp.int32), NODES, NODES),
-        in_specs=[IN_SMEM] * 2 + [IN_VMEM] * 3 + [ANYWHERE] * 3,
+        in_specs=[IN_SMEM] * 2 + [IN_VMEM] * 3 + [ANYWHERE] + [IN_VMEM] * 2,
         out_specs=(IN_VMEM, IN_SMEM, IN_VMEM, IN_VMEM),
         scratch_shapes=[
             wide(PITCH),
@@ -308,7 +303,6 @@
             pltpu.SemaphoreType.DMA,
             vmem((SIDE, SIDE, SIDE), BF16),
             pltpu.SemaphoreType.DMA((SIDE // CHUNK,)),
-            pltpu.SemaphoreType.DMA((2,)),
         ],
         compiler_params=pltpu.CompilerParams(vmem_limit_bytes=28 * MIB),
         name="first",
@@ -324,20 +318,21 @@
     )
     recv = swap(buf)
     meta = recv[:, META, :].astype(F32)
-    most = jnp.max(meta[:, CAP])
-    which = (most > FEW).astype(jnp.int32) + (most > CAP).astype(jnp.int32)
-    return recv, meta, slots, kept, which, most
+    return recv, meta, slots, kept, jnp.max(meta[:, SIDE - 1].astype(jnp.int32))
 
 
 def proceed(pitch, recv, meta, slots, source, target, tile_values):
-    lane = lax.broadcasted_iota(jnp.int32, (SIDE, CAP + 1), 1)
-    spots = meta[:, : CAP + 1] * OWN + meta[:, CAP + 1 :]
-    spots = jnp.where(lane == CAP, float(DUMMY), spots)
-    peers = jnp.minimum(meta[:, CAP : CAP + 1], float(CAP))
-    spots = spots.astype(jnp.int32)
-    index = [spots[:, 8 * j : 8 * j + 8].reshape(-1) for j in range(8)]
-    place = lax.broadcasted_iota(jnp.int32, (SIDE, 8), 1)
-    index.append(jnp.where((8 * place + 8).astype(F32) < peers, 1, 8 - place).reshape(-1))
+    meta = meta.T
+    row = lax.broadcasted_iota(jnp.int32, (CAP + 1, SIDE), 0)
+    spots = meta[: CAP + 1] * OWN + meta[CAP + 1 :]
+    spots = jnp.where(row == CAP, float(DUMMY), spots).astype(jnp.int32)
+    peers = jnp.minimum(meta[CAP : CAP + 1], float(CAP))
+    place, reader = row[:16], lax.broadcasted_iota(jnp.int32, (16, SIDE), 1)
+    more = (8 * place + 8).astype(F32) < peers
+    onward = jnp.where(reader == SIDE - 1, GROUPS, reader + 1)
+    onward = jnp.where(more, (place + 1) * SIDE + reader, onward)
+    onward = jnp.where(place >= 8, GROUPS, onward)
+    index = [spots[8 * j : 8 * j + 8].reshape(-1) for j in range(8)] + [onward.reshape(-1)]
     middle = pl.pallas_call(
         middle_kernel,
         out_shape=buffer(pitch),
@@ -423,14 +418,14 @@
 
 
 def shards(*args):
-    recv, meta, slots, nodes, which, most = begin(*args)
+    recv, meta, slots, nodes, which = begin(*args)
     onward = recv, meta, slots, *nodes, args[2]
     return lax.switch(
         which,
         [
             lambda: proceed(OWN + FEW, *onward),
             lambda: proceed(PITCH, *onward),
-            lambda: general(*args[:6], jnp.where(most > 0, args[6], 0)),
+            lambda: general(*args[:6], jnp.where(which >= 0, args[6], 0)),
         ],
     )
 

time: 199 us -> 194 us (0.975); the launches traced: 202 us -> 193 us
  blocking collectives: 172 us -> 164 us
    all_to_all x4, blocking collectives: 172 us -> 164 us  [swap(): lax.all_to_all(value, 'rows', split_axis=0, concat_axis=0, tiled=True)]
where the time goes in v5:
time: 194 us; the launch traced here: 193 us
  blocking collectives  164 us (85%)
  Pallas kernels  25.8 us (13%)
  between operations  1.94 us (1%)
    all_to_all x4, blocking collectives, swap(): lax.all_to_all(value, 'rows', split_axis=0, concat_axis=0, tiled=True)  164 us
    pallas_call x2, Pallas kernels, proceed(): recv = swap(middle(*index, recv))  12.1 us
    pallas_call x2, Pallas kernels, proceed(): pl.pallas_call(functools.partial(tail_kernel, last, pitch), out_shape=(NO...  8.34 us
    pallas_call x1, Pallas kernels, begin(): pl.pallas_call(first_kernel, out_shape=(buffer(PITCH), jax.ShapeDtypeStru...  5.37 us

profile of v5, /device:TPU:0, one launch (start us, length us, event | category | flops | bytes accessed | tf_op | source)
XLA Modules:
  0.0 192.9 jit_solution(8068118895627862101)
XLA Ops:
  1.3 0.0 copy-start.8
  1.3 5.4 %first.1 = (bf16[128,80,128]{2,1,0:T(8,128)(2,1)S(1)}, s32[8,128]{1,0:T(8,128)S(1)}, bf16[2048,128]{1,0:T(8,128)(2,1)S(1)}, bf16[2048,128]{1,0:T(8,128)(2,1)}) custom-call(s32[1]{0:T(128)S(6)} %copy.64.count, s32[128]{0:T(128)} %rows.1, s32[1,128]{1,0:T(1,128)} %bitcast.117, s32[1,128]{1,0:T(1,128)} %need_ref.1, s32[1,128]{1,0:T(1,128)} %bitcast.116, ...), custom_call_target="tpu_custom_call" | custom-call | tf_op jit(solution)/shard_map/first/pallas_call | solution.py:294
  6.7 49.0 %all_to_all.50 = bf16[128,80,128]{2,1,0:T(8,128)(2,1)S(1)} all-to-all(bf16[128,80,128]{2,1,0:T(8,128)(2,1)S(1)} %get-tuple-element.372), channel_id=1, replica_groups=mesh['rows'=128] {'rows'}, dimensions={0} | all-to-all | bytes 5242880 | tf_op jit(solution)/shard_map/all_to_all | solution.py:290
  55.6 0.1 slice_convert_fusion.1
  55.7 0.8 fusion.21
  57.1 0.0 copy-done.8
  57.1 135.9 %conditional.1 = ((bf16[2048,128]{1,0:T(8,128)(2,1)}, bf16[2048,128]{1,0:T(8,128)(2,1)})) conditional(s32[]{:T(128)} %clamp.3, (f32[128,128]{1,0:T(8,128)S(1)}, bf16[128,80,128]{2,1,0:T(8,128)(2,1)S(1)}, s32[8,128]{1,0:T(8,128)S(1)}, bf16[128,128,128]{2,1,0:T(8,128)(2,1)}, bf16[2048,128]{1,0:T(8,128)(2,1)S(1)}, ...), branch_computations={%region_1.2_spmd, %region_2.3_spmd, %region_3.14_spmd} | conditional | flops 548417344 | bytes 118714216 | solution.py:423
  57.2 0.1 copy.24
  57.3 0.1 fusion.5
  57.4 0.1 select_bitcast_fusion.refs_8_
  57.4 0.0 copy-start
  57.4 0.0 copy-start.2
  57.4 6.4 %middle.4 = bf16[128,72,128]{2,1,0:T(8,128)(2,1)S(1)} custom-call(s32[1024]{0:T(1024)S(1)} %get-tuple-element.550.refs_0_, s32[1024]{0:T(1024)S(1)} %get-tuple-element.549.refs_1_, s32[1024]{0:T(1024)S(1)} %get-tuple-element.548.refs_2_, s32[1024]{0:T(1024)S(1)} %get-tuple-element.547.refs_3_, s32[1024]{0:T(1024)S(1)} %get-tuple-element.546.refs_4_, ...), custom_call_target="tpu_custom_call" | custom-call | tf_op jit(solution)/shard_map/cond/branch_0_fun/middle/pallas_call | solution.py:350
  63.9 37.6 %all_to_all.44.recv = bf16[128,72,128]{2,1,0:T(8,128)(2,1)S(1)} all-to-all(bf16[128,72,128]{2,1,0:T(8,128)(2,1)S(1)} %middle.4), channel_id=1, replica_groups=mesh['rows'=128] {'rows'}, dimensions={0} | all-to-all | bytes 4718592 | tf_op jit(solution)/shard_map/cond/branch_0_fun/all_to_all | solution.py:290
  101.5 0.0 copy-done
  101.5 0.0 copy-done.2
  101.5 4.3 %tail.2 = bf16[128,72,128]{2,1,0:T(8,128)(2,1)S(1)} custom-call(s32[8,128]{1,0:T(8,128)S(1)} %get-tuple-element.314.slots, bf16[128,72,128]{2,1,0:T(8,128)(2,1)S(1)} %all_to_all.44.recv, bf16[128,128,128]{2,1,0:T(8,128)(2,1)S(1)} %copy-done, bf16[2048,128]{1,0:T(8,128)(2,1)S(1)} %get-tuple-element.318.source, bf16[2048,128]{1,0:T(8,128)(2,1)S(1)} %copy-done.2), custom_call_target="tpu_custom_call" | custom-call | tf_op jit(solution)/shard_map/cond/branch_0_fun/tail/pallas_call | solution.py:352
  105.8 39.9 %all_to_all.45.refs_9_ = bf16[128,72,128]{2,1,0:T(8,128)(2,1)S(1)} all-to-all(bf16[128,72,128]{2,1,0:T(8,128)(2,1)S(1)} %tail.2), channel_id=1, replica_groups=mesh['rows'=128] {'rows'}, dimensions={0} | all-to-all | bytes 4718592 | tf_op jit(solution)/shard_map/cond/branch_0_fun/all_to_all | solution.py:290
  145.7 5.6 %middle.5 = bf16[128,72,128]{2,1,0:T(8,128)(2,1)S(1)} custom-call(s32[1024]{0:T(1024)S(1)} %get-tuple-element.550.refs_0_, s32[1024]{0:T(1024)S(1)} %get-tuple-element.549.refs_1_, s32[1024]{0:T(1024)S(1)} %get-tuple-element.548.refs_2_, s32[1024]{0:T(1024)S(1)} %get-tuple-element.547.refs_3_, s32[1024]{0:T(1024)S(1)} %get-tuple-element.546.refs_4_, ...), custom_call_target="tpu_custom_call" | custom-call | tf_op jit(solution)/shard_map/cond/branch_0_fun/middle/pallas_call | solution.py:350
  151.3 37.6 %all_to_all.46.recv = bf16[128,72,128]{2,1,0:T(8,128)(2,1)S(1)} all-to-all(bf16[128,72,128]{2,1,0:T(8,128)(2,1)S(1)} %middle.5), channel_id=1, replica_groups=mesh['rows'=128] {'rows'}, dimensions={0} | all-to-all | bytes 4718592 | tf_op jit(solution)/shard_map/cond/branch_0_fun/all_to_all | solution.py:290
  188.9 4.0 %last.2 = (bf16[2048,128]{1,0:T(8,128)(2,1)}, bf16[2048,128]{1,0:T(8,128)(2,1)}) custom-call(s32[8,128]{1,0:T(8,128)S(1)} %get-tuple-element.314.slots, bf16[128,72,128]{2,1,0:T(8,128)(2,1)S(1)} %all_to_all.46.recv, bf16[128,128,128]{2,1,0:T(8,128)(2,1)S(1)} %copy-done, bf16[2048,128]{1,0:T(8,128)(2,1)S(1)} %get-tuple-element.318.source, ...), custom_call_target="tpu_custom_call" | custom-call | tf_op jit(solution)/shard_map/cond/branch_0_fun/last/pallas_call | solution.py:352
  (8 shorter events, 0.0 us)
Async XLA Ops:
  1.3 55.8 %copy-start.8 = (s32[1,128]{1,0:T(1,128)S(1)}, s32[1,128]{1,0:T(1,128)}, u32[]{:S(2)}) copy-start(s32[1,128]{1,0:T(1,128)} %need_ref.1) | copy-start | bytes 1540
  57.4 44.1 %copy-start = (bf16[128,128,128]{2,1,0:T(8,128)(2,1)S(1)}, bf16[128,128,128]{2,1,0:T(8,128)(2,1)}, u32[]{:S(2)}) copy-start(bf16[128,128,128]{2,1,0:T(8,128)(2,1)} %get-tuple-element.317.tiles) | copy-start | bytes 12582916 | tf_op jit(solution)/shard_map/cond
  57.4 44.1 %copy-start.2 = (bf16[2048,128]{1,0:T(8,128)(2,1)S(1)}, bf16[2048,128]{1,0:T(8,128)(2,1)}, u32[]{:S(2)}) copy-start(bf16[2048,128]{1,0:T(8,128)(2,1)} %get-tuple-element.319.target) | copy-start | bytes 1572868 | tf_op jit(solution)/shard_map/cond

commit v6 on v5

--- a/solution.py
+++ b/solution.py
@@ -64,8 +64,8 @@
     return lax.dot_general(tile, y, (((0,), (0,)), ((), ())), preferred_element_type=F32)
 
 
-STEP = 8
-CHUNK = 16
+STEP = 32
+CHUNK = 32
 
 
 def tile_copy(tiles, held, sems, c):

time: 194 us -> 189 us (0.974)
  blocking collectives: 164 us -> 160 us
    all_to_all x4, blocking collectives: 164 us -> 160 us  [swap(): lax.all_to_all(value, 'rows', split_axis=0, concat_axis=0, tiled=True)]
where the time goes in v6:
time: 189 us; the launch traced here: 188 us
  blocking collectives  160 us (85%)
  Pallas kernels  25.4 us (13%)
  between operations  1.94 us (1%)
    all_to_all x4, blocking collectives, swap(): lax.all_to_all(value, 'rows', split_axis=0, concat_axis=0, tiled=True)  160 us
    pallas_call x2, Pallas kernels, proceed(): recv = swap(middle(*index, recv))  12 us
    pallas_call x2, Pallas kernels, proceed(): pl.pallas_call(functools.partial(tail_kernel, last, pitch), out_shape=(NO...  8.27 us
    pallas_call x1, Pallas kernels, begin(): pl.pallas_call(first_kernel, out_shape=(buffer(PITCH), jax.ShapeDtypeStru...  5.13 us

profile of v6, /device:TPU:0, one launch (start us, length us, event | category | flops | bytes accessed | tf_op | source)
XLA Modules:
  0.0 188.3 jit_solution(3831585958221637821)
XLA Ops:
  1.3 0.0 copy-start.8
  1.3 5.1 %first.1 = (bf16[128,80,128]{2,1,0:T(8,128)(2,1)S(1)}, s32[8,128]{1,0:T(8,128)S(1)}, bf16[2048,128]{1,0:T(8,128)(2,1)S(1)}, bf16[2048,128]{1,0:T(8,128)(2,1)}) custom-call(s32[1]{0:T(128)S(6)} %copy.64.count, s32[128]{0:T(128)} %rows.1, s32[1,128]{1,0:T(1,128)} %bitcast.117, s32[1,128]{1,0:T(1,128)} %need_ref.1, s32[1,128]{1,0:T(1,128)} %bitcast.116, ...), custom_call_target="tpu_custom_call" | custom-call | tf_op jit(solution)/shard_map/first/pallas_call | solution.py:294
  6.4 46.7 %all_to_all.50 = bf16[128,80,128]{2,1,0:T(8,128)(2,1)S(1)} all-to-all(bf16[128,80,128]{2,1,0:T(8,128)(2,1)S(1)} %get-tuple-element.372), channel_id=1, replica_groups=mesh['rows'=128] {'rows'}, dimensions={0} | all-to-all | bytes 5242880 | tf_op jit(solution)/shard_map/all_to_all | solution.py:290
  53.1 0.1 slice_convert_fusion.1
  53.2 0.8 fusion.21
  54.6 0.0 copy-done.8
  54.6 133.7 %conditional.1 = ((bf16[2048,128]{1,0:T(8,128)(2,1)}, bf16[2048,128]{1,0:T(8,128)(2,1)})) conditional(s32[]{:T(128)} %clamp.3, (f32[128,128]{1,0:T(8,128)S(1)}, bf16[128,80,128]{2,1,0:T(8,128)(2,1)S(1)}, s32[8,128]{1,0:T(8,128)S(1)}, bf16[128,128,128]{2,1,0:T(8,128)(2,1)}, bf16[2048,128]{1,0:T(8,128)(2,1)S(1)}, ...), branch_computations={%region_1.2_spmd, %region_2.3_spmd, %region_3.14_spmd} | conditional | flops 548417344 | bytes 118714216 | solution.py:423
  54.7 0.1 copy.24
  54.8 0.1 fusion.5
  54.9 0.1 select_bitcast_fusion.refs_8_
  55.0 0.0 copy-start
  55.0 0.0 copy-start.2
  55.0 6.4 %middle.4 = bf16[128,72,128]{2,1,0:T(8,128)(2,1)S(1)} custom-call(s32[1024]{0:T(1024)S(1)} %get-tuple-element.550.refs_0_, s32[1024]{0:T(1024)S(1)} %get-tuple-element.549.refs_1_, s32[1024]{0:T(1024)S(1)} %get-tuple-element.548.refs_2_, s32[1024]{0:T(1024)S(1)} %get-tuple-element.547.refs_3_, s32[1024]{0:T(1024)S(1)} %get-tuple-element.546.refs_4_, ...), custom_call_target="tpu_custom_call" | custom-call | tf_op jit(solution)/shard_map/cond/branch_0_fun/middle/pallas_call | solution.py:350
  61.4 37.6 %all_to_all.44.recv = bf16[128,72,128]{2,1,0:T(8,128)(2,1)S(1)} all-to-all(bf16[128,72,128]{2,1,0:T(8,128)(2,1)S(1)} %middle.4), channel_id=1, replica_groups=mesh['rows'=128] {'rows'}, dimensions={0} | all-to-all | bytes 4718592 | tf_op jit(solution)/shard_map/cond/branch_0_fun/all_to_all | solution.py:290
  99.0 0.0 copy-done
  99.0 0.0 copy-done.2
  99.0 4.4 %tail.2 = bf16[128,72,128]{2,1,0:T(8,128)(2,1)S(1)} custom-call(s32[8,128]{1,0:T(8,128)S(1)} %get-tuple-element.314.slots, bf16[128,72,128]{2,1,0:T(8,128)(2,1)S(1)} %all_to_all.44.recv, bf16[128,128,128]{2,1,0:T(8,128)(2,1)S(1)} %copy-done, bf16[2048,128]{1,0:T(8,128)(2,1)S(1)} %get-tuple-element.318.source, bf16[2048,128]{1,0:T(8,128)(2,1)S(1)} %copy-done.2), custom_call_target="tpu_custom_call" | custom-call | tf_op jit(solution)/shard_map/cond/branch_0_fun/tail/pallas_call | solution.py:352
  103.4 37.9 %all_to_all.45.refs_9_ = bf16[128,72,128]{2,1,0:T(8,128)(2,1)S(1)} all-to-all(bf16[128,72,128]{2,1,0:T(8,128)(2,1)S(1)} %tail.2), channel_id=1, replica_groups=mesh['rows'=128] {'rows'}, dimensions={0} | all-to-all | bytes 4718592 | tf_op jit(solution)/shard_map/cond/branch_0_fun/all_to_all | solution.py:290
  141.3 5.6 %middle.5 = bf16[128,72,128]{2,1,0:T(8,128)(2,1)S(1)} custom-call(s32[1024]{0:T(1024)S(1)} %get-tuple-element.550.refs_0_, s32[1024]{0:T(1024)S(1)} %get-tuple-element.549.refs_1_, s32[1024]{0:T(1024)S(1)} %get-tuple-element.548.refs_2_, s32[1024]{0:T(1024)S(1)} %get-tuple-element.547.refs_3_, s32[1024]{0:T(1024)S(1)} %get-tuple-element.546.refs_4_, ...), custom_call_target="tpu_custom_call" | custom-call | tf_op jit(solution)/shard_map/cond/branch_0_fun/middle/pallas_call | solution.py:350
  146.9 37.6 %all_to_all.46.recv = bf16[128,72,128]{2,1,0:T(8,128)(2,1)S(1)} all-to-all(bf16[128,72,128]{2,1,0:T(8,128)(2,1)S(1)} %middle.5), channel_id=1, replica_groups=mesh['rows'=128] {'rows'}, dimensions={0} | all-to-all | bytes 4718592 | tf_op jit(solution)/shard_map/cond/branch_0_fun/all_to_all | solution.py:290
  184.5 3.9 %last.2 = (bf16[2048,128]{1,0:T(8,128)(2,1)}, bf16[2048,128]{1,0:T(8,128)(2,1)}) custom-call(s32[8,128]{1,0:T(8,128)S(1)} %get-tuple-element.314.slots, bf16[128,72,128]{2,1,0:T(8,128)(2,1)S(1)} %all_to_all.46.recv, bf16[128,128,128]{2,1,0:T(8,128)(2,1)S(1)} %copy-done, bf16[2048,128]{1,0:T(8,128)(2,1)S(1)} %get-tuple-element.318.source, ...), custom_call_target="tpu_custom_call" | custom-call | tf_op jit(solution)/shard_map/cond/branch_0_fun/last/pallas_call | solution.py:352
  (8 shorter events, 0.0 us)
Async XLA Ops:
  1.3 53.3 %copy-start.8 = (s32[1,128]{1,0:T(1,128)S(1)}, s32[1,128]{1,0:T(1,128)}, u32[]{:S(2)}) copy-start(s32[1,128]{1,0:T(1,128)} %need_ref.1) | copy-start | bytes 1540
  55.0 44.0 %copy-start = (bf16[128,128,128]{2,1,0:T(8,128)(2,1)S(1)}, bf16[128,128,128]{2,1,0:T(8,128)(2,1)}, u32[]{:S(2)}) copy-start(bf16[128,128,128]{2,1,0:T(8,128)(2,1)} %get-tuple-element.317.tiles) | copy-start | bytes 12582916 | tf_op jit(solution)/shard_map/cond
  55.0 44.0 %copy-start.2 = (bf16[2048,128]{1,0:T(8,128)(2,1)S(1)}, bf16[2048,128]{1,0:T(8,128)(2,1)}, u32[]{:S(2)}) copy-start(bf16[2048,128]{1,0:T(8,128)(2,1)} %get-tuple-element.319.target) | copy-start | bytes 1572868 | tf_op jit(solution)/shard_map/cond

commit v7 on v6

--- a/solution.py
+++ b/solution.py
@@ -194,16 +194,15 @@
                 window = ref.at[pl.ds(spot + (SUMS + PAD - j), 8), :]
                 pltpu.store(window, sums[j], mask=row_at == j)
 
-    def two(groups):
-        first = onward[groups[1]]
-        second = onward[first]
-        third = onward[second]
-        fourth = onward[third]
-        work(groups)
-        work((first, second))
-        return third, fourth
-
-    lax.while_loop(lambda groups: groups[0] < GROUPS, two, (jnp.int32(0), onward[0]))
+    def several(groups):
+        for _ in range(4):
+            first = onward[groups[1]]
+            later = first, onward[first]
+            work(groups)
+            groups = later
+        return groups
+
+    lax.while_loop(lambda groups: groups[0] < GROUPS, several, (jnp.int32(0), onward[0]))
 
     def narrow(d, _):
         at = pl.ds(pl.multiple_of(SUMS + PAD + d * OWN, 8), OWN)

time: 189 us -> 189 us (level)
  blocking collectives: 160 us -> 158 us
where the time goes in v7:
time: 189 us; the launch traced here: 188 us
  blocking collectives  158 us (84%)
  Pallas kernels  26.3 us (14%)
  between operations  1.94 us (1%)
    all_to_all x4, blocking collectives, swap(): lax.all_to_all(value, 'rows', split_axis=0, concat_axis=0, tiled=True)  158 us
    pallas_call x2, Pallas kernels, proceed(): recv = swap(middle(*index, recv))  11 us
    pallas_call x2, Pallas kernels, proceed(): pl.pallas_call(functools.partial(tail_kernel, last, pitch), out_shape=(NO...  9.57 us
    pallas_call x1, Pallas kernels, begin(): pl.pallas_call(first_kernel, out_shape=(buffer(PITCH), jax.ShapeDtypeStru...  5.64 us

profile of v7, /device:TPU:0, one launch (start us, length us, event | category | flops | bytes accessed | tf_op | source)
XLA Modules:
  0.0 187.9 jit_solution(4296409173836394589)
XLA Ops:
  1.3 0.0 copy-start.8
  1.3 5.6 %first.1 = (bf16[128,80,128]{2,1,0:T(8,128)(2,1)S(1)}, s32[8,128]{1,0:T(8,128)S(1)}, bf16[2048,128]{1,0:T(8,128)(2,1)S(1)}, bf16[2048,128]{1,0:T(8,128)(2,1)}) custom-call(s32[1]{0:T(128)S(6)} %copy.64.count, s32[128]{0:T(128)} %rows.1, s32[1,128]{1,0:T(1,128)} %bitcast.117, s32[1,128]{1,0:T(1,128)} %need_ref.1, s32[1,128]{1,0:T(1,128)} %bitcast.116, ...), custom_call_target="tpu_custom_call" | custom-call | tf_op jit(solution)/shard_map/first/pallas_call | solution.py:293
  6.9 46.2 %all_to_all.50 = bf16[128,80,128]{2,1,0:T(8,128)(2,1)S(1)} all-to-all(bf16[128,80,128]{2,1,0:T(8,128)(2,1)S(1)} %get-tuple-element.372), channel_id=1, replica_groups=mesh['rows'=128] {'rows'}, dimensions={0} | all-to-all | bytes 5242880 | tf_op jit(solution)/shard_map/all_to_all | solution.py:289
  53.1 0.1 slice_convert_fusion.1
  53.2 0.8 fusion.21
  54.6 0.0 copy-done.8
  54.6 133.3 %conditional.1 = ((bf16[2048,128]{1,0:T(8,128)(2,1)}, bf16[2048,128]{1,0:T(8,128)(2,1)})) conditional(s32[]{:T(128)} %clamp.3, (f32[128,128]{1,0:T(8,128)S(1)}, bf16[128,80,128]{2,1,0:T(8,128)(2,1)S(1)}, s32[8,128]{1,0:T(8,128)S(1)}, bf16[128,128,128]{2,1,0:T(8,128)(2,1)}, bf16[2048,128]{1,0:T(8,128)(2,1)S(1)}, ...), branch_computations={%region_1.2_spmd, %region_2.3_spmd, %region_3.14_spmd} | conditional | flops 548417344 | bytes 118714216 | solution.py:422
  54.6 0.1 copy.24
  54.8 0.1 fusion.5
  54.8 0.1 select_bitcast_fusion.refs_8_
  54.9 0.0 copy-start
  54.9 0.0 copy-start.2
  54.9 5.7 %middle.4 = bf16[128,72,128]{2,1,0:T(8,128)(2,1)S(1)} custom-call(s32[1024]{0:T(1024)S(1)} %get-tuple-element.550.refs_0_, s32[1024]{0:T(1024)S(1)} %get-tuple-element.549.refs_1_, s32[1024]{0:T(1024)S(1)} %get-tuple-element.548.refs_2_, s32[1024]{0:T(1024)S(1)} %get-tuple-element.547.refs_3_, s32[1024]{0:T(1024)S(1)} %get-tuple-element.546.refs_4_, ...), custom_call_target="tpu_custom_call" | custom-call | tf_op jit(solution)/shard_map/cond/branch_0_fun/middle/pallas_call | solution.py:349
  60.6 37.6 %all_to_all.44.recv = bf16[128,72,128]{2,1,0:T(8,128)(2,1)S(1)} all-to-all(bf16[128,72,128]{2,1,0:T(8,128)(2,1)S(1)} %middle.4), channel_id=1, replica_groups=mesh['rows'=128] {'rows'}, dimensions={0} | all-to-all | bytes 4718592 | tf_op jit(solution)/shard_map/cond/branch_0_fun/all_to_all | solution.py:289
  98.2 0.0 copy-done
  98.2 0.0 copy-done.2
  98.2 5.2 %tail.2 = bf16[128,72,128]{2,1,0:T(8,128)(2,1)S(1)} custom-call(s32[8,128]{1,0:T(8,128)S(1)} %get-tuple-element.314.slots, bf16[128,72,128]{2,1,0:T(8,128)(2,1)S(1)} %all_to_all.44.recv, bf16[128,128,128]{2,1,0:T(8,128)(2,1)S(1)} %copy-done, bf16[2048,128]{1,0:T(8,128)(2,1)S(1)} %get-tuple-element.318.source, bf16[2048,128]{1,0:T(8,128)(2,1)S(1)} %copy-done.2), custom_call_target="tpu_custom_call" | custom-call | tf_op jit(solution)/shard_map/cond/branch_0_fun/tail/pallas_call | solution.py:351
  103.4 37.2 %all_to_all.45.refs_9_ = bf16[128,72,128]{2,1,0:T(8,128)(2,1)S(1)} all-to-all(bf16[128,72,128]{2,1,0:T(8,128)(2,1)S(1)} %tail.2), channel_id=1, replica_groups=mesh['rows'=128] {'rows'}, dimensions={0} | all-to-all | bytes 4718592 | tf_op jit(solution)/shard_map/cond/branch_0_fun/all_to_all | solution.py:289
  140.6 5.4 %middle.5 = bf16[128,72,128]{2,1,0:T(8,128)(2,1)S(1)} custom-call(s32[1024]{0:T(1024)S(1)} %get-tuple-element.550.refs_0_, s32[1024]{0:T(1024)S(1)} %get-tuple-element.549.refs_1_, s32[1024]{0:T(1024)S(1)} %get-tuple-element.548.refs_2_, s32[1024]{0:T(1024)S(1)} %get-tuple-element.547.refs_3_, s32[1024]{0:T(1024)S(1)} %get-tuple-element.546.refs_4_, ...), custom_call_target="tpu_custom_call" | custom-call | tf_op jit(solution)/shard_map/cond/branch_0_fun/middle/pallas_call | solution.py:349
  146.0 37.6 %all_to_all.46.recv = bf16[128,72,128]{2,1,0:T(8,128)(2,1)S(1)} all-to-all(bf16[128,72,128]{2,1,0:T(8,128)(2,1)S(1)} %middle.5), channel_id=1, replica_groups=mesh['rows'=128] {'rows'}, dimensions={0} | all-to-all | bytes 4718592 | tf_op jit(solution)/shard_map/cond/branch_0_fun/all_to_all | solution.py:289
  183.5 4.4 %last.2 = (bf16[2048,128]{1,0:T(8,128)(2,1)}, bf16[2048,128]{1,0:T(8,128)(2,1)}) custom-call(s32[8,128]{1,0:T(8,128)S(1)} %get-tuple-element.314.slots, bf16[128,72,128]{2,1,0:T(8,128)(2,1)S(1)} %all_to_all.46.recv, bf16[128,128,128]{2,1,0:T(8,128)(2,1)S(1)} %copy-done, bf16[2048,128]{1,0:T(8,128)(2,1)S(1)} %get-tuple-element.318.source, ...), custom_call_target="tpu_custom_call" | custom-call | tf_op jit(solution)/shard_map/cond/branch_0_fun/last/pallas_call | solution.py:351
  (8 shorter events, 0.0 us)
Async XLA Ops:
  1.3 53.3 %copy-start.8 = (s32[1,128]{1,0:T(1,128)S(1)}, s32[1,128]{1,0:T(1,128)}, u32[]{:S(2)}) copy-start(s32[1,128]{1,0:T(1,128)} %need_ref.1) | copy-start | bytes 1540
  54.9 43.3 %copy-start = (bf16[128,128,128]{2,1,0:T(8,128)(2,1)S(1)}, bf16[128,128,128]{2,1,0:T(8,128)(2,1)}, u32[]{:S(2)}) copy-start(bf16[128,128,128]{2,1,0:T(8,128)(2,1)} %get-tuple-element.317.tiles) | copy-start | bytes 12582916 | tf_op jit(solution)/shard_map/cond
  54.9 43.3 %copy-start.2 = (bf16[2048,128]{1,0:T(8,128)(2,1)S(1)}, bf16[2048,128]{1,0:T(8,128)(2,1)}, u32[]{:S(2)}) copy-start(bf16[2048,128]{1,0:T(8,128)(2,1)} %get-tuple-element.319.target) | copy-start | bytes 1572868 | tf_op jit(solution)/shard_map/cond
